TPU v7x, 32 devices: a whole 2x2x4 slice. The times are simulated.
32 devices in a mesh: sys: 2 (over x), aux: 4 (over z), orb: 4 (over y, core).
Axes of the slice: x: 2, y: 2, z: 4, core: 2. Of those that a mesh axis runs over, the one named last changes fastest.
Arguments:
- aux_ints: float32 [1792, 320, 320], P(('sys', 'aux'), 'orb'), parts along dimension 0
- metric: float32 [1792, 896], P(('sys', 'aux')), parts along dimension 0
- orbitals: float32 [2, 320, 32], P('sys'), parts along dimension 0
Outputs:
- output: float32 [2, 320, 320], P('sys', 'orb', 'aux'), parts along dimension 0
There are 2 independent parts. A program takes and returns all parts, laid end to end along the dimension named above; each array names one.
All inputs are finite; a program needn't handle non-finite values.
Results may differ from a plain program's by a relative error of at most 0.001.
Values are sent between devices in bfloat16 or wider.
A program may use at most 1 GiB of HBM per device.

v0:
```python
import jax
import jax.numpy as jnp
from jax import lax
from jax.sharding import PartitionSpec as P

PRECISE = lax.Precision.HIGHEST


def solution(mesh):
    def local_fock(ints_blk, metric_blk, orbitals):
        m_loc = ints_blk.shape[1]
        row_start = lax.axis_index('orb') * m_loc
        half_tr = jnp.einsum('qml,dli->qmdi', ints_blk, orbitals, precision=PRECISE, preferred_element_type=jnp.float32)
        orb_rows = lax.dynamic_slice_in_dim(orbitals, row_start, m_loc, axis=1)
        gamma_part = jnp.einsum('qmdi,dmi->dq', half_tr, orb_rows, precision=PRECISE, preferred_element_type=jnp.float32)
        gamma_raw = lax.psum(gamma_part, 'orb')
        gamma_all = lax.all_gather(gamma_raw, 'aux', axis=1, tiled=True)
        gamma_fit = jnp.einsum('dq,pq->dp', gamma_all, metric_blk, precision=PRECISE, preferred_element_type=jnp.float32)
        weight_part = jnp.dot(gamma_fit, metric_blk, precision=PRECISE, preferred_element_type=jnp.float32)
        weights = lax.psum_scatter(weight_part, 'aux', scatter_dimension=1, tiled=True)
        coulomb = jnp.einsum('dq,qmn->dmn', weights, ints_blk, precision=PRECISE, preferred_element_type=jnp.float32)
        half_all = lax.all_gather(half_tr, 'aux', axis=0, tiled=True)
        fitted = jnp.einsum('pq,qmdi->pmdi', metric_blk, half_all, precision=PRECISE, preferred_element_type=jnp.float32)
        fitted_all = lax.all_gather(fitted, 'orb', axis=1, tiled=True)
        exchange = jnp.einsum('pmdi,pndi->dmn', fitted, fitted_all, precision=PRECISE, preferred_element_type=jnp.float32)
        fock_part = 2.0 * coulomb - exchange
        return lax.psum_scatter(fock_part, 'aux', scatter_dimension=2, tiled=True)

    return jax.shard_map(local_fock, mesh=mesh, in_specs=(P(('sys', 'aux'), 'orb', None), P(('sys', 'aux'), None), P('sys', None, None)), out_specs=P('sys', 'orb', 'aux'), check_vma=False)
```

profile of v0, /device:TPU:0, one launch (start us, length us, event | category | flops | bytes accessed | tf_op | source)
XLA Modules:
  0.0 430.1 jit_solution(305073321051168125)
XLA Ops:
  6.5 19.3 %fusion.26 = f32[224,80,32]{0,2,1:T(8,128)S(1)} fusion(f32[224,80,320]{0,2,1:T(8,128)} %param.3, f32[1,320,32]{1,2,0:T(8,128)} %param.5), kind=kOutput, calls=%fused_computation.16 | convolution fusion | flops 2202009600 | bytes 25272320 | tf_op jit(solution)/shard_map/qml,dli->qmdi/dot_general | solution.py:13
  25.9 3.9 copy.13
  29.8 0.0 all-gather.5.cloned.1.call-update
  29.8 0.0 reduce-scatter.7.cloned.1.call-start
  29.9 0.6 dynamic-slice
  31.1 0.8 constant_dynamic-slice_fusion
  32.0 2.8 fusion.20
  34.7 8.4 %psum.7 = f32[1,224]{1,0:T(1,128)S(1)} all-reduce(f32[1,224]{1,0:T(1,128)S(1)} %fusion.20), channel_id=1, replica_groups=mesh['sys'=2,'aux'=4,'orb'=4] {'orb'}, use_global_device_ids=true, to_apply=%region_0.0 | all-reduce | flops 224 | bytes 1792 | tf_op jit(solution)/shard_map/psum | solution.py:16
  43.2 0.2 dynamic-update-slice
  43.4 12.2 %all-reduce = f32[896]{0:T(1024)S(1)} all-reduce(f32[896]{0:T(1024)S(1)} %dynamic-update-slice), channel_id=1, replica_groups=mesh['sys'=2,'aux'=4,'orb'=4] {'aux'}, use_global_device_ids=true, to_apply=%add | all-reduce | flops 896 | bytes 7168 | tf_op jit(solution)/shard_map/reshape.5
  55.6 0.8 convolution_bitcast_fusion.2
  56.4 2.4 convolution_bitcast_fusion.1
  58.8 0.2 all-gather.7.cloned.1.call-start
  59.1 227.1 %all-gather.5.cloned.1.call-done = f32[896,80,32]{1,2,0:T(8,128)} async-done(((f32[224,80,32]{1,2,0:T(8,128)}), f32[896,80,32]{1,2,0:T(8,128)}) %all-gather.5.cloned.1.call-update) | async-done | bytes 9175056 | tf_op jit(solution)/shard_map/all_gather | solution.py:22
  286.2 14.0 %copy.9 = f32[896,80,32]{0,2,1:T(8,128)} copy(f32[896,80,32]{1,2,0:T(8,128)} %all-gather.5.cloned.1.call-done) | data formatting | bytes 18350080 | tf_op jit(solution)/shard_map/all_gather | solution.py:22
  300.2 12.1 %convolution_bitcast_fusion = f32[224,80,32]{0,2,1:T(8,128)} fusion(f32[896,80,32]{0,2,1:T(8,128)} %copy.9, f32[224,896]{1,0:T(8,128)S(1)} %copy-done), kind=kOutput, calls=%fused_computation.5 | convolution fusion | flops 6165626880 | bytes 12271616 | tf_op jit(solution)/shard_map/pq,qmdi->pmdi/dot_general | solution.py:23
  312.4 0.0 reduce-scatter.9.cloned.1.call-start
  312.4 0.0 reduce-scatter.7.cloned.1.call-done
  312.4 26.8 %fusion.24 = f32[1,80,320]{2,0,1:T(1,128)S(1)} fusion(f32[224,80,320]{0,2,1:T(8,128)} %param.3, f32[224,1]{1,0:T(8,128)} %reduce-scatter.7.cloned.1.call-done), kind=kOutput, calls=%fused_computation.14 | convolution fusion | flops 68812800 | bytes 23040896 | tf_op jit(solution)/shard_map/dq,qmn->dmn/dot_general | solution.py:21
  339.2 42.0 %all-gather.7.cloned.1.call-done = f32[224,320,32]{0,2,1:T(8,128)} async-done(((f32[224,80,32]{0,2,1:T(8,128)}), f32[224,320,32]{0,2,1:T(8,128)}) %all-gather.7.cloned.1.call-update) | async-done | bytes 9175056 | tf_op jit(solution)/shard_map/all_gather | solution.py:24
  381.2 19.6 %fusion.15 = f32[1,80,320]{2,1,0:T(8,128)} fusion(f32[224,320,32]{0,2,1:T(8,128)} %all-gather.7.cloned.1.call-done, f32[224,80,32]{0,2,1:T(8,128)S(1)} %copy-done.1, f32[1,80,320]{2,0,1:T(1,128)S(1)} %fusion.24), kind=kOutput, calls=%fused_computation.9 | convolution fusion | flops 2202060800 | bytes 11673600 | tf_op jit(solution)/shard_map/pmdi,pndi->dmn/dot_general | solution.py:25
  400.8 1.7 copy.20
  402.5 19.6 %reduce-scatter.9.cloned.1.call-done = f32[80,80]{1,0:T(8,128)} async-done(((f32[320,80]{1,0:T(8,128)}), f32[80,80]{1,0:T(8,128)}) %reduce-scatter.9.cloned.1.call-update) | async-done | bytes 25616
  422.1 1.5 copy.21
  (12 shorter events, 0.1 us)
Async XLA Ops:
  6.5 49.1 %copy-start = (f32[224,896]{1,0:T(8,128)S(1)}, f32[224,896]{1,0:T(8,128)}, u32[]{:S(2)}) copy-start(f32[224,896]{1,0:T(8,128)} %param.4) | copy-start | bytes 2408452
  6.5 279.7 %all-gather.5.cloned.1.call-start = ((), (), s32[]{:S(2)}) async-start(), calls=%async_computation.2 | async-start | bytes 18350080 | tf_op jit(solution)/shard_map/all_gather | solution.py:22
  25.9 4.0 copy-start.2
  29.8 282.6 %reduce-scatter.7.cloned.1.call-start = ((), (), s32[]{:S(2)}) async-start(), calls=%async_computation.4 | async-start | bytes 573440
  58.8 322.4 %all-gather.7.cloned.1.call-start = ((), (), s32[]{:S(2)}) async-start(), calls=%async_computation.3 | async-start | bytes 13107200 | tf_op jit(solution)/shard_map/all_gather | solution.py:24
  312.3 68.9 %copy-start.1 = (f32[224,80,32]{0,2,1:T(8,128)S(1)}, f32[224,80,32]{0,2,1:T(8,128)}, u32[]{:S(2)}) copy-start(f32[224,80,32]{0,2,1:T(8,128)} %convolution_bitcast_fusion) | copy-start | bytes 6881284
  312.4 109.7 %reduce-scatter.9.cloned.1.call-start = ((), (), s32[]{:S(2)}) async-start(), calls=%async_computation.5 | async-start | bytes 204800
Sparse Core Ops, SparseCore 0:
  30.0 256.2 all-gather.4
  288.5 19.5 reduce-scatter.6
  312.5 68.7 all-gather.6
  402.6 19.4 reduce-scatter.8
where the time goes:
time: 431 us; the launch traced here: 430 us
  waiting for transfers between devices  289 us (67%)
  matrix products  83.7 us (19%)
  local copies, waits for them, and re-layouts  22.8 us (5%)
  blocking collectives  20.6 us (5%)
  between operations  13.8 us (3%)
    all_gather x1, waiting for transfers between devices, local_fock(): half_all = lax.all_gather(half_tr, 'aux', axis=0, tiled=True)  227 us
    all_gather x1, waiting for transfers between devices, local_fock(): fitted_all = lax.all_gather(fitted, 'orb', axis=1, tiled=True)  42 us
    dot_general x1, matrix products, local_fock(): jnp.einsum('dq,qmn->dmn', weights, ints_blk, precision=PRECISE, preferred...  26.8 us
    unnamed x6, waiting for transfers between devices  19.7 us
    dot_general x1, matrix products, local_fock(): jnp.einsum('pmdi,pndi->dmn', fitted, fitted_all, precision=PRECISE, prefe...  19.6 us
    dot_general x1, matrix products, local_fock(): jnp.einsum('qml,dli->qmdi', ints_blk, orbitals, precision=PRECISE, prefer...  19.3 us
    all_gather x1, local copies, waits for them, and re-layouts, local_fock(): half_all = lax.all_gather(half_tr, 'aux', axis=0, tiled=True)  14 us
    another operation x1, blocking collectives  12.2 us
  transfers between devices with their start and end apart: 4, of which 3 were waited for; matrix products, arithmetic and copies ran while one was open for 14% of the time, Pallas kernels for 0%

commit v1 on v0

v1 whole, which is shorter than its diff:
```python
import jax
import jax.numpy as jnp
from jax import lax
from jax.sharding import PartitionSpec as P

PRECISE = lax.Precision.HIGHEST


def solution(mesh):
    n_aux, n_orb = mesh.shape['aux'], mesh.shape['orb']
    n_dev = n_aux * n_orb

    def local_fock(ints_blk, metric_blk, orbitals):
        q_loc, m_loc, n_bas = ints_blk.shape
        occ = orbitals.shape[2]
        coeff = orbitals[0]
        metric_all = lax.all_gather(metric_blk.astype(jnp.bfloat16), 'aux', axis=0, tiled=True)
        row_start = lax.axis_index('orb') * m_loc
        half_tr = jnp.einsum('qml,li->qmi', ints_blk, coeff, precision=PRECISE, preferred_element_type=jnp.float32)
        orb_rows = lax.dynamic_slice_in_dim(coeff, row_start, m_loc, axis=0)
        gamma_part = jnp.sum(half_tr * orb_rows[None], axis=(1, 2))[None]
        packed = jnp.transpose(half_tr, (2, 1, 0)).astype(jnp.bfloat16).reshape(n_dev, occ // n_dev, m_loc, q_loc)
        moved = lax.all_to_all(packed, ('aux', 'orb'), split_axis=0, concat_axis=0, tiled=True)
        gamma_raw = lax.psum(gamma_part, 'orb')
        gamma_all = lax.all_gather(gamma_raw, 'aux', axis=1, tiled=True)
        gamma_fit = jnp.einsum('dq,pq->dp', gamma_all, metric_blk, precision=PRECISE, preferred_element_type=jnp.float32)
        weight_part = jnp.dot(gamma_fit, metric_blk, precision=PRECISE, preferred_element_type=jnp.float32)
        weights = lax.psum_scatter(weight_part, 'aux', scatter_dimension=1, tiled=True)
        coulomb = jnp.einsum('dq,qmn->mn', weights, ints_blk, precision=PRECISE, preferred_element_type=jnp.float32)
        moved = moved.reshape(n_aux, n_orb, occ // n_dev, m_loc, q_loc)
        fitted = jnp.einsum('aoimq,aqp->iomp', moved.astype(jnp.float32),
                            metric_all.astype(jnp.float32).reshape(n_aux, q_loc, -1),
                            precision=PRECISE, preferred_element_type=jnp.float32)
        fitted = fitted.reshape(occ // n_dev, n_orb * m_loc, -1)
        exchange = jnp.einsum('imp,inp->mn', fitted, fitted, precision=PRECISE, preferred_element_type=jnp.float32)
        fock = lax.dynamic_update_slice_in_dim(
            -exchange, lax.dynamic_slice_in_dim(-exchange, row_start, m_loc, axis=0) + 2.0 * coulomb, row_start, axis=0)
        fock = lax.psum_scatter(fock, 'orb', scatter_dimension=0, tiled=True)
        return lax.psum_scatter(fock, 'aux', scatter_dimension=1, tiled=True)[None]

    return jax.shard_map(local_fock, mesh=mesh, in_specs=(P(('sys', 'aux'), 'orb', None), P(('sys', 'aux'), None), P('sys', None, None)), out_specs=P('sys', 'orb', 'aux'), check_vma=False)
```

time: 431 us -> 179 us (0.42)
  waiting for transfers between devices: 289 us -> 75.7 us
  matrix products: 83.7 us -> 56.6 us
  local copies, waits for them, and re-layouts: 22.8 us -> 7.53 us
    all_gather x2 -> x1, waiting for transfers between devices: 269 us -> 17.8 us  [local_fock(): lax.all_gather(metric_blk.astype(jnp.bfloat16), 'aux', axis=0, tiled=True)]
    dot_general x5 -> x4, matrix products: 80.5 us -> 53.3 us  [the longest x1 26.6 us: local_fock(): jnp.einsum('dq,qmn->mn', weights, ints_blk, precision=PRECISE, preferred_...]
    reduce_scatter x0 -> x1, waiting for transfers between devices: none -> 20.5 us  [local_fock(): fock = lax.psum_scatter(fock, 'orb', scatter_dimension=0, tiled=True)]
    unnamed x6, waiting for transfers between devices: 19.7 us -> 37.4 us
    all_gather x1 -> x0, local copies, waits for them, and re-layouts: 14 us -> none  [local_fock(): half_all = lax.all_gather(half_tr, 'aux', axis=0, tiled=True)]
  transfers between devices with their start and end apart: 4 -> 5, of which waited for: 3 -> 4; matrix products, arithmetic and copies ran while one was open for 14% -> 16% of each run, Pallas kernels for 0% -> 0%
where the time goes in v1:
time: 179 us
  waiting for transfers between devices  75.7 us (42%)
  matrix products  56.6 us (32%)
  blocking collectives  20.4 us (11%)
  between operations  13.9 us (8%)
  local copies, waits for them, and re-layouts  7.53 us (4%)
  starting transfers between devices  4.01 us (2%)
    unnamed x6, waiting for transfers between devices  37.4 us
    dot_general x1, matrix products, local_fock(): jnp.einsum('dq,qmn->mn', weights, ints_blk, precision=PRECISE, preferred_...  26.6 us
    reduce_scatter x1, waiting for transfers between devices, local_fock(): fock = lax.psum_scatter(fock, 'orb', scatter_dimension=0, tiled=True)  20.5 us
    dot_general x1, matrix products, local_fock(): jnp.einsum('qml,li->qmi', ints_blk, coeff, precision=PRECISE, preferred_e...  19.9 us
    all_gather x1, waiting for transfers between devices, local_fock(): lax.all_gather(metric_blk.astype(jnp.bfloat16), 'aux', axis=0, tiled=True)  17.8 us
    another operation x1, blocking collectives  11.9 us
    psum x1, blocking collectives, local_fock(): gamma_raw = lax.psum(gamma_part, 'orb')  8.44 us
    unnamed x13, local copies, waits for them, and re-layouts  5.57 us
  transfers between devices with their start and end apart: 5, of which 4 were waited for; matrix products, arithmetic and copies ran while one was open for 16% of the time, Pallas kernels for 0%

profile of v1, /device:TPU:0, one launch (start us, length us, event | category | flops | bytes accessed | tf_op | source)
XLA Modules:
  0.0 178.9 jit_solution(8196191568195507342)
XLA Ops:
  6.5 0.8 copy-done
  7.3 0.1 dynamic-slice_bitcast_fusion
  7.4 0.1 copy.13
  7.5 19.9 %multiply_reduce_fusion = (f32[224]{0:T(256)S(1)}, bf16[32,80,224]{2,0,1:T(8,128)(2,1)S(1)}) fusion(f32[80,32]{1,0:T(8,128)S(1)} %copy.13, f32[224,80,320]{0,2,1:T(8,128)} %param.3, f32[1,320,32]{1,2,0:T(8,128)S(1)} %copy-done), kind=kOutput, calls=%fused_computation | convolution fusion | flops 2203729664 | bytes 24136576 | tf_op jit(solution)/shard_map/qml,li->qmi/dot_general | solution.py:19
  27.4 8.4 %psum.7 = f32[1,224]{1,0:T(1,128)S(1)} all-reduce(f32[1,224]{1,0:T(1,128)S(1)} %bitcast.64), channel_id=1, replica_groups=mesh['sys'=2,'aux'=4,'orb'=4] {'orb'}, use_global_device_ids=true, to_apply=%region_1.0 | all-reduce | flops 224 | bytes 1792 | tf_op jit(solution)/shard_map/psum | solution.py:24
  35.9 0.6 dynamic-slice.1
  37.1 0.2 dynamic-update-slice
  37.4 11.9 %all-reduce = f32[896]{0:T(1024)S(1)} all-reduce(f32[896]{0:T(1024)S(1)} %dynamic-update-slice), channel_id=1, replica_groups=mesh['sys'=2,'aux'=4,'orb'=4] {'aux'}, use_global_device_ids=true, to_apply=%add | all-reduce | flops 896 | bytes 7168 | tf_op jit(solution)/shard_map/reshape.2
  49.3 0.8 convolution_bitcast_fusion.2
  50.1 2.4 %convolution_bitcast_fusion.1 = f32[896,1]{1,0:T(8,128)} fusion(f32[224,1]{0,1:T(1,128)S(1)} %convolution_bitcast_fusion.2, f32[224,896]{1,0:T(8,128)S(1)} %copy-done.1), kind=kOutput, calls=%fused_computation.6 | convolution fusion | flops 2408448 | bytes 807296
  52.6 0.8 convert_element_type.13
  53.4 1.8 %copy.18 = bf16[32,80,224]{2,1,0:T(8,128)(2,1)} copy(bf16[32,80,224]{2,0,1:T(8,128)(2,1)S(1)} %get-tuple-element.6) | data formatting | bytes 2293760 | tf_op jit(solution)/shard_map/reshape | solution.py:22
  55.2 3.7 %all-to-all-start = ((bf16[16,2,80,224]{3,2,1,0:T(8,128)(2,1)}), bf16[16,2,80,224]{3,2,1,0:T(8,128)(2,1)S(1)}, u32[]{:S(2)}, u32[]{:S(2)}) async-start(bf16[16,2,80,224]{3,2,1,0:T(8,128)(2,1)} %bitcast.3), calls=%async_computation | async-start | bytes 2621440 | tf_op jit(solution)/shard_map/all_to_all | solution.py:23
  58.9 0.2 reduce-scatter.8.cloned.1.call-start
  59.1 17.5 %reduce-scatter.10.cloned.1.call-done = f32[224,1]{1,0:T(8,128)} async-done(((f32[896,1]{1,0:T(8,128)}), f32[224,1]{1,0:T(8,128)}) %reduce-scatter.10.cloned.1.call-update) | async-done | bytes 912
  76.6 26.6 %fusion.5 = f32[1,80,320]{2,0,1:T(1,128)S(1)} fusion(f32[224,80,320]{0,2,1:T(8,128)} %param.3, f32[224,1]{1,0:T(8,128)} %reduce-scatter.10.cloned.1.call-done), kind=kOutput, calls=%fused_computation.11 | convolution fusion | flops 68812800 | bytes 23040896 | tf_op jit(solution)/shard_map/dq,qmn->mn/dot_general | solution.py:29
  103.3 17.8 %all-gather.2.cloned.1.call-done = bf16[896,896]{1,0:T(8,128)(2,1)} async-done(((bf16[224,896]{1,0:T(8,128)(2,1)}), bf16[896,896]{1,0:T(8,128)(2,1)}) %all-gather.2.cloned.1.call-update) | async-done | bytes 1605648 | tf_op jit(solution)/shard_map/all_gather | solution.py:17
  121.0 2.9 %fusion = f32[4,2,80,896,1]{3,2,0,1,4:T(8,128)S(1)} fusion(bf16[4,224,896,1,1]{2,1,3,4,0:T(8,128)(2,1)} %bitcast.66, bf16[4,4,2,80,224]{4,3,2,1,0:T(8,128)(2,1)S(1)} %bitcast.61), kind=kOutput, calls=%fused_computation.1 | convolution fusion | flops 1027604480 | bytes 5046272 | tf_op jit(solution)/shard_map/aoimq,aqp->iomp/dot_general | solution.py:31
  124.0 3.9 %fusion.2 = f32[320,320]{1,0:T(8,128)S(1)} fusion(f32[2,320,896]{2,1,0:T(8,128)S(1)} %bitcast.60), kind=kOutput, calls=%fused_computation.5 | convolution fusion | flops 2202112000 | bytes 2703360 | tf_op jit(solution)/shard_map/imp,inp->mn/dot_general | solution.py:35
  127.9 0.8 copy-done.2
  128.8 20.5 %reduce-scatter.8.cloned.1.call-done = f32[80,320]{1,0:T(8,128)} async-done(((f32[320,320]{1,0:T(8,128)}), f32[80,320]{1,0:T(8,128)}) %reduce-scatter.8.cloned.1.call-update) | async-done | bytes 102416 | tf_op jit(solution)/shard_map/reduce_scatter | solution.py:38
  149.3 1.7 copy.22
  151.0 19.9 %reduce-scatter.12.cloned.1.call-done = f32[80,80]{1,0:T(8,128)} async-done(((f32[320,80]{1,0:T(8,128)}), f32[80,80]{1,0:T(8,128)}) %reduce-scatter.12.cloned.1.call-update) | async-done | bytes 25616
  170.8 1.5 copy.23
  (17 shorter events, 0.2 us)
Async XLA Ops:
  6.5 0.8 copy-start
  6.5 70.1 %reduce-scatter.10.cloned.1.call-start = ((), (), s32[]{:S(2)}) async-start(), calls=%async_computation.6 | async-start | bytes 573440
  7.5 28.4 %copy-start.3 = (u32[32]{0:T(128)S(1)}, u32[32]{0:T(128)}, u32[]{:S(2)}) copy-start(u32[32]{0:T(128)} %constant.18) | copy-start | bytes 388
  7.5 41.8 %copy-start.1 = (f32[224,896]{1,0:T(8,128)S(1)}, f32[224,896]{1,0:T(8,128)}, u32[]{:S(2)}) copy-start(f32[224,896]{1,0:T(8,128)} %param.4) | copy-start | bytes 2408452
  52.5 68.5 %all-gather.2.cloned.1.call-start = ((), (), s32[]{:S(2)}) async-start(), calls=%async_computation.4 | async-start | bytes 2007040 | tf_op jit(solution)/shard_map/all_gather | solution.py:17
  55.2 48.1 %all-to-all-start = ((bf16[16,2,80,224]{3,2,1,0:T(8,128)(2,1)}), bf16[16,2,80,224]{3,2,1,0:T(8,128)(2,1)S(1)}, u32[]{:S(2)}, u32[]{:S(2)}) async-start(bf16[16,2,80,224]{3,2,1,0:T(8,128)(2,1)} %bitcast.3), calls=%async_computation | async-start | bytes 2621440 | tf_op jit(solution)/shard_map/all_to_all | solution.py:23
  58.9 90.4 %reduce-scatter.8.cloned.1.call-start = ((), (), s32[]{:S(2)}) async-start(), calls=%async_computation.5 | async-start | bytes 614400 | tf_op jit(solution)/shard_map/reduce_scatter | solution.py:38
  127.9 0.8 copy-start.2
  128.7 42.1 %reduce-scatter.12.cloned.1.call-start = ((), (), s32[]{:S(2)}) async-start(), calls=%async_computation.7 | async-start | bytes 204800
Sparse Core Ops, SparseCore 0:
  52.7 23.9 reduce-scatter.9
  78.2 42.7 all-gather.1
  128.8 20.4 reduce-scatter.7
  151.4 19.4 reduce-scatter.11

commit v2 on v0

v2 whole, which is shorter than its diff:
```python
import functools

import jax
import jax.numpy as jnp
from jax import lax
from jax.experimental import pallas as pl
from jax.experimental.pallas import tpu as pltpu
from jax.sharding import PartitionSpec as P

F32, BF16 = jnp.float32, jnp.bfloat16
MESH = pl.DeviceIdType.MESH
NT = (((1,), (1,)), ((), ()))
AHEAD = 3
SLOTS = 4


def split3(x):
    h0 = x.astype(BF16)
    r1 = x - h0.astype(F32)
    h1 = r1.astype(BF16)
    r2 = r1 - h1.astype(F32)
    return h0, h1, r2.astype(BF16)


def dot(a, b):
    return jnp.dot(a, b, preferred_element_type=F32)


def dot_nt(a, b):
    return lax.dot_general(a, b, NT, preferred_element_type=F32)


def kernel(b_hbm, m_hbm, c_ref, out_ref, bb, b3, stage, sbuf, rbuf, mall, mown, cb, c3, tt, ks, jacc, gam, gsend, grecv,
           fsend, frecv, wb, gs, gr, b_sem, m_sem, s_send, s_recv, mz_send, mz_recv, mf_send, mf_recv, g_send, g_recv,
           f_send, f_recv, r_send, r_recv):
    a, o = lax.axis_index('aux'), lax.axis_index('orb')
    me = a * 4 + o
    planes = [(a + 2) % 4, 3 - a, a + 1 - 2 * (a % 2), a]
    peers = [(planes[k // 4], (o + k % 4) % 4) for k in range(16) if k != 12]

    def remote(src, dst, send, recv, dest):
        return pltpu.make_async_remote_copy(src_ref=src, dst_ref=dst, send_sem=send, recv_sem=recv,
                                            device_id={'aux': dest[0], 'orb': dest[1]}, device_id_type=MESH)

    def b_copies(g):
        slot = lax.rem(g, SLOTS)
        rows = pl.ds(pl.multiple_of(g * 8, 8), 8)
        return [pltpu.make_async_copy(b_hbm.at[:, rows, pl.ds(0, 128)], bb.at[0, g], b_sem.at[0, slot]),
                pltpu.make_async_copy(b_hbm.at[:, rows, pl.ds(128, 128)], bb.at[1, g], b_sem.at[1, slot]),
                pltpu.make_async_copy(b_hbm.at[:, rows, pl.ds(256, 64)], b3.at[slot], b_sem.at[2, slot])]

    for g in range(AHEAD):
        for cp in b_copies(g):
            cp.start()
    m_copy = pltpu.make_async_copy(m_hbm, mown, m_sem)
    m_copy.start()

    barrier = pltpu.get_barrier_semaphore()
    for dest in peers:
        pl.semaphore_signal(barrier, inc=1, device_id={'aux': dest[0], 'orb': dest[1]}, device_id_type=MESH)

    ct = jnp.transpose(c_ref[...])
    parts = split3(ct)
    zero64 = jnp.zeros((32, 64), BF16)
    zero256 = jnp.zeros((32, 256), BF16)
    for k in range(3):
        head, tail = parts[k][:, :256], parts[k][:, 256:]
        heads = [head if j <= 2 - k else zero256 for j in range(3)]
        tails = [tail if j <= 2 - k else zero64 for j in range(3)]
        c3[32 * k:32 * k + 32, :] = jnp.concatenate(heads + tails + [zero64], axis=1)
    own = jnp.transpose(c_ref[pl.ds(pl.multiple_of(o * 80, 8), 80), :])
    for m in range(80):
        cb[m] = jnp.broadcast_to(own[:, m:m + 1], (32, 128))
    stage[1] = jnp.zeros((512, 128), F32)
    gam[...] = jnp.zeros((32, 256), F32)

    m_copy.wait()
    m0, m1, m2 = split3(mown[...])
    pad = jnp.zeros((32, 896), BF16)
    mall[pl.ds(a, 1), 0:224, :] = m0[None]
    mall[pl.ds(a, 1), 224:256, :] = pad[None]
    mall[4, 0:224, :] = m1
    mall[4, 224:256, :] = pad
    mall[5, 0:224, :] = m2
    mall[5, 224:256, :] = pad

    pl.semaphore_wait(barrier, 15)

    quarter = pl.ds(pl.multiple_of(o * 64, 64), 64)

    def mz_copy(j):
        return remote(mall.at[a, quarter, :], mall.at[a, quarter, :], mz_send.at[j], mz_recv.at[a], (planes[j], o))

    for j in range(3):
        mz_copy(j).start()

    def mf_copy(j, k):
        part = mall.at[planes[j], quarter, :]
        return remote(part, part, mf_send.at[j, k], mf_recv.at[planes[j], o], (a, (o + k + 1) % 4))

    def half_copy(ii, dest, rows):
        d = dest[0] * 4 + dest[1]
        return remote(sbuf.at[2 * d + ii, rows, :], rbuf.at[ii, me, rows, :], s_send.at[ii, d], s_recv.at[ii, me], dest)

    def group(g, carry):
        for cp in b_copies(g):
            cp.wait()

        @pl.when(g + AHEAD < 10)
        def _():
            for cp in b_copies(g + AHEAD):
                cp.start()

        slot = lax.rem(g, SLOTS)
        b_tail = bb.at[2, g].reshape(1792, 128)
        b_tail[:, 0:64] = b3.at[slot].reshape(1792, 64)[...]
        views = [bb.at[t, g].reshape(1792, 128) for t in range(3)]
        base = lax.rem(g, 2) * 8

        def row(m, carry):
            x0, x1, x2 = [split3(v[pl.ds(m, 224, stride=8), :]) for v in views]
            z = jnp.zeros((224, 64), BF16)
            w = jnp.concatenate([x0[0], x1[0], x0[1], x1[1], x0[2], x1[2],
                                 x2[0][:, :64], x2[1][:, :64], x2[2][:, :64], z], axis=1)
            r = dot_nt(c3[...], w)
            h = r[0:32] + r[32:64] + r[64:96]
            stage[0, pl.ds(base + m, 32, stride=16), :] = h[:, :128]
            stage[1, pl.ds(base + m, 32, stride=16), 0:96] = h[:, 128:]
            coef = cb[g * 8 + m]
            gam[:, 0:128] += h[:, :128] * coef
            gam[:, 128:224] += h[:, 128:] * coef[:, :96]
            return carry

        lax.fori_loop(0, 8, row, 0)

        @pl.when(lax.rem(g, 2) == 1)
        def _():
            rows = pl.ds(pl.multiple_of((g // 2) * 16, 16), 16)
            for t in range(2):
                sbuf[:, rows, 128 * t:128 * t + 128] = stage[t].reshape(32, 16, 128).astype(BF16)
            for dest in peers:
                half_copy(0, dest, rows).start()

        @pl.when(g == 3)
        def _():
            for j in range(3):
                remote(mall.at[planes[j], quarter, :], mall.at[planes[j], quarter, :], mz_send.at[j],
                       mz_recv.at[planes[j]], (planes[j], o)).wait_recv()
                for k in range(3):
                    mf_copy(j, k).start()

        return carry

    lax.fori_loop(0, 10, group, 0)

    full = pl.ds(0, 80)
    for dest in peers:
        half_copy(1, dest, full).start()
    rbuf[:, pl.ds(me, 1)] = sbuf[pl.ds(2 * me, 2)][:, None]

    def g_copy(dest):
        return remote(gsend, grecv.at[me], g_send.at[dest[0] * 4 + dest[1]], g_recv.at[me], dest)

    g_row = jnp.sum(gam[...], axis=0, keepdims=True)
    gsend[...] = g_row
    grecv[pl.ds(me, 1)] = g_row[None]
    for dest in peers:
        g_copy(dest).start()

    def lanes_of(rows):
        return jnp.concatenate([r[:, :224] for r in rows], axis=1)

    def times_metric(row):
        return jnp.sum(mown[...] * row, axis=1, keepdims=True)

    for s in peers:
        remote(gsend, grecv.at[s[0] * 4 + s[1]], g_send.at[0], g_recv.at[s[0] * 4 + s[1]], s).wait_recv()
    gamma = lanes_of([grecv[4 * b] + grecv[4 * b + 1] + grecv[4 * b + 2] + grecv[4 * b + 3] for b in range(4)])
    fit = jnp.broadcast_to(times_metric(gamma), (224, 128))
    fit_row = jnp.concatenate([jnp.transpose(fit[:128])[0:1], jnp.transpose(fit[96:])[0:1, 32:], jnp.zeros((1, 32), F32)],
                              axis=1)
    fsend[...] = fit_row
    frecv[pl.ds(a, 1)] = fit_row[None]

    def f_copy(j):
        return remote(fsend, frecv.at[a], f_send.at[j], f_recv.at[a], (planes[j], o))

    for j in range(3):
        f_copy(j).start()
    for j in range(3):
        remote(fsend, frecv.at[planes[j]], f_send.at[j], f_recv.at[planes[j]], (planes[j], o)).wait_recv()
    weights = times_metric(lanes_of([frecv[b] for b in range(4)]))
    wb[...] = jnp.broadcast_to(2.0 * weights, (224, 128))

    def coul(q, acc):
        w = jnp.broadcast_to(wb[pl.ds(q, 1), :], (8, 128))
        return tuple(acc[t * 10 + g] + w * bb[t, g, q] for t in range(3) for g in range(10))

    acc = lax.fori_loop(0, 224, coul, tuple(jnp.zeros((8, 128), F32) for _ in range(30)))
    for g in range(10):
        jacc[8 * g:8 * g + 8, :] = jnp.concatenate([acc[g], acc[10 + g], acc[20 + g][:, :64]], axis=1)

    for j in range(3):
        for k in range(3):
            po = (o + k + 1) % 4
            part = mall.at[planes[j], pl.ds(pl.multiple_of(po * 64, 64), 64), :]
            remote(part, part, mf_send.at[j, k], mf_recv.at[planes[j], po], (a, po)).wait_recv()

    for ii in range(2):
        for s in peers:
            n = s[0] * 4 + s[1]
            remote(sbuf.at[ii], rbuf.at[ii, n], s_send.at[ii, n], s_recv.at[ii, n], s).wait_recv()
        for n0, n1 in ((0, 256), (256, 512), (512, 768), (768, 896)):
            t = dot(rbuf[ii, 0:4].reshape(320, 256), mall[0, :, n0:n1])
            for b in range(1, 4):
                t += dot(rbuf[ii, 4 * b:4 * b + 4].reshape(320, 256), mall[b, :, n0:n1])
            mine = rbuf[ii, pl.ds(a * 4, 4)].reshape(320, 256)
            t += dot(mine, mall[4, :, n0:n1]) + dot(mine, mall[5, :, n0:n1])
            for k, h in enumerate(split3(t)):
                tt[k, :, n0:n1] = h
        t0, t1, t2 = tt[0], tt[1], tt[2]
        k = dot_nt(t0, t0) + dot_nt(t1, t1) + dot_nt(t0, t1) + dot_nt(t0, t2) + dot_nt(t1, t0) + dot_nt(t2, t0)
        if ii == 0:
            ks[...] = k
        else:
            ks[...] += k

    for c in range(4):
        gs[:, c] = -ks[:, 80 * c:80 * c + 80].reshape(4, 80, 80)
        gs[pl.ds(o, 1), c] += jacc[:, 80 * c:80 * c + 80][None]

    def r_copy(dest):
        return remote(gs.at[dest[1], dest[0]], gr.at[me], r_send.at[dest[0] * 4 + dest[1]], r_recv.at[me], dest)

    for dest in peers:
        r_copy(dest).start()
    total = gs[o, a]
    for s in peers:
        n = s[0] * 4 + s[1]
        remote(gs.at[s[1], s[0]], gr.at[n], r_send.at[n], r_recv.at[n], s).wait_recv()
        total = total + gr[n]
    out_ref[0] = total

    for dest in peers:
        half_copy(0, dest, full).wait_send()
        half_copy(1, dest, full).wait_send()
        g_copy(dest).wait_send()
        r_copy(dest).wait_send()
    for j in range(3):
        mz_copy(j).wait_send()
        f_copy(j).wait_send()
        for k in range(3):
            mf_copy(j, k).wait_send()


def solution(mesh):
    def local_fock(ints_blk, metric_blk, orbitals):
        dma = pltpu.SemaphoreType.DMA
        return pl.pallas_call(
            kernel,
            name='fock',
            out_shape=jax.ShapeDtypeStruct((1, 80, 80), F32),
            in_specs=[pl.BlockSpec(memory_space=pl.ANY), pl.BlockSpec(memory_space=pl.ANY),
                      pl.BlockSpec(memory_space=pltpu.VMEM)],
            out_specs=pl.BlockSpec(memory_space=pltpu.VMEM),
            scratch_shapes=[
                pltpu.VMEM((3, 10, 224, 8, 128), F32),
                pltpu.VMEM((SLOTS, 224, 8, 64), F32),
                pltpu.VMEM((2, 512, 128), F32),
                pltpu.VMEM((32, 80, 256), BF16),
                pltpu.VMEM((2, 16, 80, 256), BF16),
                pltpu.VMEM((6, 256, 896), BF16),
                pltpu.VMEM((224, 896), F32),
                pltpu.VMEM((80, 32, 128), F32),
                pltpu.VMEM((96, 1024), BF16),
                pltpu.VMEM((3, 320, 896), BF16),
                pltpu.VMEM((320, 320), F32),
                pltpu.VMEM((80, 320), F32),
                pltpu.VMEM((32, 256), F32),
                pltpu.VMEM((1, 256), F32),
                pltpu.VMEM((16, 1, 256), F32),
                pltpu.VMEM((1, 256), F32),
                pltpu.VMEM((4, 1, 256), F32),
                pltpu.VMEM((224, 128), F32),
                pltpu.VMEM((4, 4, 80, 80), F32),
                pltpu.VMEM((16, 80, 80), F32),
                dma((3, SLOTS)), dma(()),
                dma((2, 16)), dma((2, 16)),
                dma((3,)), dma((4,)),
                dma((3, 3)), dma((4, 4)),
                dma((16,)), dma((16,)),
                dma((3,)), dma((4,)),
                dma((16,)), dma((16,)),
            ],
            compiler_params=pltpu.CompilerParams(collective_id=0, has_side_effects=True, vmem_limit_bytes=67043328),
        )(ints_blk, metric_blk, orbitals[0])

    return jax.shard_map(local_fock, mesh=mesh, in_specs=(P(('sys', 'aux'), 'orb', None), P(('sys', 'aux'), None), P('sys', None, None)), out_specs=P('sys', 'orb', 'aux'), check_vma=False)
```

time: 431 us -> 120 us (0.28)
  waiting for transfers between devices: 289 us -> 0 us
  Pallas kernels: 0 us -> 87.1 us
  matrix products: 83.7 us -> 0 us
  blocking collectives: 20.6 us -> 0 us
  between operations: 13.8 us -> 0.01 us
  local copies, waits for them, and re-layouts: 22.8 us -> 31.3 us
    all_gather x2 -> x0, waiting for transfers between devices: 269 us -> none  [the longest x1 227 us: local_fock(): half_all = lax.all_gather(half_tr, 'aux', axis=0, tiled=True)]
    pallas_call x0 -> x1, Pallas kernels: none -> 87.1 us  [local_fock(): pl.pallas_call(kernel, name='fock', out_shape=jax.ShapeDtypeStruct((1, 80...]
    dot_general x6 -> x0, matrix products: 81.3 us -> none  [the longest x1 26.8 us: local_fock(): jnp.einsum('dq,qmn->dmn', weights, ints_blk, precision=PRECISE, preferred...]
    unnamed x11 -> x3, local copies, waits for them, and re-layouts: 3.99 us -> 31.3 us
    unnamed x6 -> x0, waiting for transfers between devices: 19.7 us -> none
    all_gather x1 -> x0, local copies, waits for them, and re-layouts: 14 us -> none  [local_fock(): half_all = lax.all_gather(half_tr, 'aux', axis=0, tiled=True)]
    another operation x1 -> x0, blocking collectives: 12.2 us -> none
    psum x1 -> x0, blocking collectives: 8.41 us -> none  [local_fock(): gamma_raw = lax.psum(gamma_part, 'orb')]
  transfers between devices with their start and end apart: 4 -> 0, of which waited for: 3 -> 0; matrix products, arithmetic and copies ran while one was open for 14% -> 0% of each run, Pallas kernels for 0% -> 0%
where the time goes in v2:
time: 120 us; the launch traced here: 118 us
  Pallas kernels  87.1 us (73%)
  local copies, waits for them, and re-layouts  31.3 us (26%)
    pallas_call x1, Pallas kernels, local_fock(): pl.pallas_call(kernel, name='fock', out_shape=jax.ShapeDtypeStruct((1, 80...  87.1 us
    unnamed x3, local copies, waits for them, and re-layouts  31.3 us

profile of v2, /device:TPU:0, one launch (start us, length us, event | category | flops | bytes accessed | tf_op | source)
XLA Modules:
  0.0 118.4 jit_solution(4672050525897028583)
XLA Ops:
  0.0 1.6 %copy.4 = f32[1,320,32]{2,1,0:T(8,128)} copy(f32[1,320,32]{1,2,0:T(8,128)} %param.5) | data formatting | bytes 81920 | tf_op args[2]
  1.6 28.3 %copy.5.b_hbm = f32[224,80,320]{2,1,0:T(8,128)} copy(f32[224,80,320]{0,2,1:T(8,128)} %param.3) | data formatting | bytes 45875200 | tf_op args[0]
  29.9 87.1 %fock.1 = f32[1,80,80]{2,1,0:T(8,128)} custom-call(f32[224,80,320]{2,1,0:T(8,128)} %copy.5.b_hbm, f32[224,896]{1,0:T(8,128)} %m_hbm.1, f32[320,32]{1,0:T(8,128)} %bitcast.1), custom_call_target="tpu_custom_call" | custom-call | tf_op jit(solution)/shard_map/fock/pallas_call | solution.py:259
  117.0 1.4 %copy.7 = f32[1,80,80]{2,1,0:T(8,128)} copy(f32[1,80,80]{2,1,0:T(8,128)} %fock.1) | data formatting | bytes 51200

commit v3 on v2

v3 whole, which is shorter than its diff:
```python
import functools

import jax
import jax.numpy as jnp
from jax import lax
from jax.experimental import pallas as pl
from jax.experimental.pallas import tpu as pltpu
from jax.sharding import PartitionSpec as P

F32, BF16 = jnp.float32, jnp.bfloat16
MESH = pl.DeviceIdType.MESH
NT = (((1,), (1,)), ((), ()))
AHEAD = 4


def split3(x):
    h0 = x.astype(BF16)
    r1 = x - h0.astype(F32)
    h1 = r1.astype(BF16)
    r2 = r1 - h1.astype(F32)
    return h0, h1, r2.astype(BF16)


def dot(a, b):
    return jnp.dot(a, b, preferred_element_type=F32)


def dot_nt(a, b):
    return lax.dot_general(a, b, NT, preferred_element_type=F32)


def kernel(b_hbm, m_hbm, c_ref, out_ref, bb, stage, sbuf, rbuf, mall, mown, cb, c3, tt, ks, jacc, gam, gsend, grecv,
           fsend, frecv, gs, gr, b_sem, m_sem, s_send, s_recv, mz_send, mz_recv, mf_send, mf_recv, g_send, g_recv,
           f_send, f_recv, r_send, r_recv):
    a, o = lax.axis_index('aux'), lax.axis_index('orb')
    me = a * 4 + o
    planes = [(a + 2) % 4, 3 - a, a + 1 - 2 * (a % 2), a]
    peers = [(planes[k // 4], (o + k % 4) % 4) for k in range(16) if k != 12]

    def remote(src, dst, send, recv, dest):
        return pltpu.make_async_remote_copy(src_ref=src, dst_ref=dst, send_sem=send, recv_sem=recv,
                                            device_id={'aux': dest[0], 'orb': dest[1]}, device_id_type=MESH)

    def b_copy(g):
        rows = pl.ds(g * 4, 4)
        return pltpu.make_async_copy(b_hbm.at[rows], bb.at[rows], b_sem.at[g])

    for g in range(AHEAD):
        b_copy(g).start()
    m_copy = pltpu.make_async_copy(m_hbm, mown, m_sem)
    m_copy.start()

    barrier = pltpu.get_barrier_semaphore()
    for dest in peers:
        pl.semaphore_signal(barrier, inc=1, device_id={'aux': dest[0], 'orb': dest[1]}, device_id_type=MESH)

    parts = split3(c_ref[...])
    zero = jnp.zeros((32, 320), BF16)
    for k in range(3):
        rows = [parts[k] if j <= 2 - k else zero for j in range(3)]
        c3[32 * k:32 * k + 32, :] = jnp.concatenate(rows + [zero[:, :64]], axis=1)
    own = jnp.zeros((32, 80), F32)
    for k in range(4):
        own = jnp.where(o == k, c_ref[:, 80 * k:80 * k + 80], own)
    for m in range(80):
        cb[m] = jnp.broadcast_to(own[:, m:m + 1], (32, 128))
    stage[1] = jnp.zeros((512, 128), F32)
    gam[...] = jnp.zeros((32, 256), F32)

    m_copy.wait()
    m0, m1, m2 = split3(mown[...])
    pad = jnp.zeros((32, 896), BF16)
    mall[pl.ds(a, 1), 0:224, :] = m0[None]
    mall[pl.ds(a, 1), 224:256, :] = pad[None]
    mall[4, 0:224, :] = m1
    mall[4, 224:256, :] = pad
    mall[5, 0:224, :] = m2
    mall[5, 224:256, :] = pad

    pl.semaphore_wait(barrier, 15)

    quarter = pl.ds(pl.multiple_of(o * 64, 64), 64)

    def mz_copy(plane, step):
        part = mall.at[plane, quarter, :]
        return remote(part, part, mz_send.at[plane, (step + 1) // 2], mz_recv.at[plane], (a + step, o))

    def relay(r, action):
        for step in (1, -1):
            plane = a - step * r

            @pl.when((plane >= 0) & (plane <= 3))
            def _():
                if action == 'send' and r > 0:
                    mz_copy(plane, step).wait_recv()

                @pl.when((a + step >= 0) & (a + step <= 3))
                def _():
                    if r < 3:
                        cp = mz_copy(plane, step)
                        cp.start() if action == 'send' else cp.wait_send()

    relay(0, 'send')

    def mf_copy(j, k):
        part = mall.at[planes[j], quarter, :]
        return remote(part, part, mf_send.at[j, k], mf_recv.at[planes[j], o], (a, (o + k + 1) % 4))

    def half_copy(ii, dest, rows):
        d = dest[0] * 4 + dest[1]
        return remote(sbuf.at[2 * d + ii, rows, :], rbuf.at[ii, me, rows, :], s_send.at[ii, d], s_recv.at[ii, me], dest)

    def group(g, carry):
        for k in range(2):
            b_copy(2 * g + k).wait()

        @pl.when(2 * g + AHEAD < 20)
        def _():
            for k in range(2):
                b_copy(2 * g + k + AHEAD).start()

        base = lax.rem(g, 2) * 8

        def row(m, carry):
            w = jnp.concatenate(list(split3(bb[g * 8 + m])) + [jnp.zeros((64, 224), BF16)], axis=0)
            r = dot(c3[...], w)
            h = r[0:32] + r[32:64] + r[64:96]
            stage[0, pl.ds(base + m, 32, stride=16), :] = h[:, :128]
            stage[1, pl.ds(base + m, 32, stride=16), 0:96] = h[:, 128:]
            coef = cb[g * 8 + m]
            gam[:, 0:128] += h[:, :128] * coef
            gam[:, 128:224] += h[:, 128:] * coef[:, :96]
            return carry

        lax.fori_loop(0, 8, row, 0)

        @pl.when(lax.rem(g, 2) == 1)
        def _():
            rows = pl.ds(pl.multiple_of((g // 2) * 16, 16), 16)
            for t in range(2):
                sbuf[:, rows, 128 * t:128 * t + 128] = stage[t].reshape(32, 16, 128).astype(BF16)
            for dest in peers:
                half_copy(0, dest, rows).start()

        for r in (1, 2):
            @pl.when(g == 4 * r)
            def _():
                relay(r, 'send')

        return carry

    lax.fori_loop(0, 10, group, 0)

    def g_copy(dest):
        return remote(gsend, grecv.at[me], g_send.at[dest[0] * 4 + dest[1]], g_recv.at[me], dest)

    g_row = jnp.sum(gam[...], axis=0, keepdims=True)
    gsend[...] = g_row
    grecv[pl.ds(me, 1)] = g_row[None]
    for dest in peers:
        g_copy(dest).start()

    full = pl.ds(0, 80)
    for dest in peers:
        half_copy(1, dest, full).start()
    rbuf[:, pl.ds(me, 1)] = sbuf[pl.ds(2 * me, 2)][:, None]

    relay(3, 'send')
    for j in range(3):
        for k in range(3):
            mf_copy(j, k).start()

    def lanes_of(rows):
        return jnp.concatenate([r[:, :224] for r in rows], axis=1)

    def as_row(col):
        x = jnp.broadcast_to(col, (224, 128))
        return jnp.concatenate([jnp.transpose(x[:128])[0:1], jnp.transpose(x[96:])[0:1, 32:], jnp.zeros((1, 32), F32)],
                               axis=1)

    def times_metric(row):
        return jnp.sum(mown[...] * row, axis=1, keepdims=True)

    for s in peers:
        remote(gsend, grecv.at[s[0] * 4 + s[1]], g_send.at[0], g_recv.at[s[0] * 4 + s[1]], s).wait_recv()
    gamma = lanes_of([grecv[4 * b] + grecv[4 * b + 1] + grecv[4 * b + 2] + grecv[4 * b + 3] for b in range(4)])
    fit_row = as_row(times_metric(gamma))
    fsend[...] = fit_row
    frecv[pl.ds(a, 1)] = fit_row[None]

    def f_copy(j):
        return remote(fsend, frecv.at[a], f_send.at[j], f_recv.at[a], (planes[j], o))

    for j in range(3):
        f_copy(j).start()
    for j in range(3):
        remote(fsend, frecv.at[planes[j]], f_send.at[j], f_recv.at[planes[j]], (planes[j], o)).wait_recv()
    weights = times_metric(lanes_of([frecv[b] for b in range(4)]))
    w_row = as_row(2.0 * weights)

    lane = lax.broadcasted_iota(jnp.int32, (320, 80), 1)

    def coul(m, acc):
        x = bb[m]
        col = jnp.sum(x[:, :128] * w_row[:, :128], axis=1, keepdims=True) + jnp.sum(
            x[:, 128:] * w_row[:, 128:224], axis=1, keepdims=True)
        return jnp.where(lane == m, col, acc)

    jacc[...] = lax.fori_loop(0, 80, coul, jnp.zeros((320, 80), F32))
    jt = jnp.transpose(jacc[...])

    for j in range(3):
        for k in range(3):
            po = (o + k + 1) % 4
            part = mall.at[planes[j], pl.ds(pl.multiple_of(po * 64, 64), 64), :]
            remote(part, part, mf_send.at[j, k], mf_recv.at[planes[j], po], (a, po)).wait_recv()

    for ii in range(2):
        for s in peers:
            n = s[0] * 4 + s[1]
            remote(sbuf.at[ii], rbuf.at[ii, n], s_send.at[ii, n], s_recv.at[ii, n], s).wait_recv()
        for n0, n1 in ((0, 256), (256, 512), (512, 768), (768, 896)):
            t = dot(rbuf[ii, 0:4].reshape(320, 256), mall[0, :, n0:n1])
            for b in range(1, 4):
                t += dot(rbuf[ii, 4 * b:4 * b + 4].reshape(320, 256), mall[b, :, n0:n1])
            mine = rbuf[ii, pl.ds(a * 4, 4)].reshape(320, 256)
            t += dot(mine, mall[4, :, n0:n1]) + dot(mine, mall[5, :, n0:n1])
            for k, h in enumerate(split3(t)):
                tt[k, :, n0:n1] = h
        t0, t1, t2 = tt[0], tt[1], tt[2]
        k = dot_nt(t0, t0) + dot_nt(t1, t1) + dot_nt(t0, t1) + dot_nt(t0, t2) + dot_nt(t1, t0) + dot_nt(t2, t0)
        if ii == 0:
            ks[...] = k
        else:
            ks[...] += k

    for c in range(4):
        gs[:, c] = -ks[:, 80 * c:80 * c + 80].reshape(4, 80, 80)
        gs[pl.ds(o, 1), c] += jt[:, 80 * c:80 * c + 80][None]

    def r_copy(dest):
        return remote(gs.at[dest[1], dest[0]], gr.at[me], r_send.at[dest[0] * 4 + dest[1]], r_recv.at[me], dest)

    for dest in peers:
        r_copy(dest).start()
    total = gs[o, a]
    for s in peers:
        n = s[0] * 4 + s[1]
        remote(gs.at[s[1], s[0]], gr.at[n], r_send.at[n], r_recv.at[n], s).wait_recv()
        total = total + gr[n]
    out_ref[0] = total

    for dest in peers:
        half_copy(0, dest, full).wait_send()
        half_copy(1, dest, full).wait_send()
        g_copy(dest).wait_send()
        r_copy(dest).wait_send()
    for r in range(3):
        relay(r, 'drain')
    for j in range(3):
        f_copy(j).wait_send()
        for k in range(3):
            mf_copy(j, k).wait_send()


def solution(mesh):
    def local_fock(ints_blk, metric_blk, orbitals):
        dma = pltpu.SemaphoreType.DMA
        return pl.pallas_call(
            kernel,
            name='fock',
            out_shape=jax.ShapeDtypeStruct((1, 80, 80), F32),
            in_specs=[pl.BlockSpec(memory_space=pl.ANY), pl.BlockSpec(memory_space=pl.ANY),
                      pl.BlockSpec(memory_space=pltpu.VMEM)],
            out_specs=pl.BlockSpec(memory_space=pltpu.VMEM),
            scratch_shapes=[
                pltpu.VMEM((80, 320, 224), F32),
                pltpu.VMEM((2, 512, 128), F32),
                pltpu.VMEM((32, 80, 256), BF16),
                pltpu.VMEM((2, 16, 80, 256), BF16),
                pltpu.VMEM((6, 256, 896), BF16),
                pltpu.VMEM((224, 896), F32),
                pltpu.VMEM((80, 32, 128), F32),
                pltpu.VMEM((96, 1024), BF16),
                pltpu.VMEM((3, 320, 896), BF16),
                pltpu.VMEM((320, 320), F32),
                pltpu.VMEM((320, 80), F32),
                pltpu.VMEM((32, 256), F32),
                pltpu.VMEM((1, 256), F32),
                pltpu.VMEM((16, 1, 256), F32),
                pltpu.VMEM((1, 256), F32),
                pltpu.VMEM((4, 1, 256), F32),
                pltpu.VMEM((4, 4, 80, 80), F32),
                pltpu.VMEM((16, 80, 80), F32),
                dma((20,)), dma(()),
                dma((2, 16)), dma((2, 16)),
                dma((4, 2)), dma((4,)),
                dma((3, 3)), dma((4, 4)),
                dma((16,)), dma((16,)),
                dma((3,)), dma((4,)),
                dma((16,)), dma((16,)),
            ],
            compiler_params=pltpu.CompilerParams(collective_id=0, has_side_effects=True, vmem_limit_bytes=67043328),
        )(jnp.transpose(ints_blk, (1, 2, 0)), metric_blk, jnp.transpose(orbitals[0]))

    return jax.shard_map(local_fock, mesh=mesh, in_specs=(P(('sys', 'aux'), 'orb', None), P(('sys', 'aux'), None), P('sys', None, None)), out_specs=P('sys', 'orb', 'aux'), check_vma=False)
```

time: 120 us -> 85.5 us (0.71)
  local copies, waits for them, and re-layouts: 31.3 us -> 1.4 us
  Pallas kernels: 87.1 us -> 82.7 us
    unnamed x3 -> x1, local copies, waits for them, and re-layouts: 31.3 us -> 1.4 us
    pallas_call x1, Pallas kernels: 87.1 us -> 82.7 us  [local_fock(): pl.pallas_call(kernel, name='fock', out_shape=jax.ShapeDtypeStruct((1, 80...]
where the time goes in v3:
time: 85.5 us; the launch traced here: 84.1 us
  Pallas kernels  82.7 us (97%)
  local copies, waits for them, and re-layouts  1.4 us (2%)
    pallas_call x1, Pallas kernels, local_fock(): pl.pallas_call(kernel, name='fock', out_shape=jax.ShapeDtypeStruct((1, 80...  82.7 us

profile of v3, /device:TPU:0, one launch (start us, length us, event | category | flops | bytes accessed | tf_op | source)
XLA Modules:
  0.0 84.1 jit_solution(17092508111523995516)
XLA Ops:
  0.0 82.7 %fock.1 = f32[1,80,80]{2,1,0:T(8,128)} custom-call(f32[80,320,224]{2,1,0:T(8,128)} %bitcast.4, f32[224,896]{1,0:T(8,128)} %m_hbm.1, f32[32,320]{1,0:T(8,128)} %bitcast.5), custom_call_target="tpu_custom_call" | custom-call | tf_op jit(solution)/shard_map/fock/pallas_call | solution.py:269
  82.7 1.4 %copy.5 = f32[1,80,80]{2,1,0:T(8,128)} copy(f32[1,80,80]{2,1,0:T(8,128)} %fock.1) | data formatting | bytes 51200

commit v4 on v3

v4 whole, which is shorter than its diff:
```python
import functools

import jax
import jax.numpy as jnp
from jax import lax
from jax.experimental import pallas as pl
from jax.experimental.pallas import tpu as pltpu
from jax.sharding import PartitionSpec as P

F32, BF16 = jnp.float32, jnp.bfloat16
MESH = pl.DeviceIdType.MESH
NT = (((1,), (1,)), ((), ()))
AHEAD = 4


def split3(x):
    h0 = x.astype(BF16)
    r1 = x - h0.astype(F32)
    h1 = r1.astype(BF16)
    r2 = r1 - h1.astype(F32)
    return h0, h1, r2.astype(BF16)


def dot(a, b):
    return jnp.dot(a, b, preferred_element_type=F32)


def dot_nt(a, b):
    return lax.dot_general(a, b, NT, preferred_element_type=F32)


def kernel(b_hbm, m_hbm, c_ref, out_ref, bb, stage, sbuf, rbuf, mall, mown, cb, c3, tt, ks, jacc, gam, gsend, grecv,
           fsend, frecv, gs, gp, gf, gr, b_sem, m_sem, s_send, s_recv, mz_send, mz_recv, mf_send, mf_recv, g_send, g_recv,
           f_send, f_recv, p_sems, r_send, r_recv):
    a, o = lax.axis_index('aux'), lax.axis_index('orb')
    me = a * 4 + o
    core, row_y = o % 2, o // 2
    core_mate, y_mate = o + 1 - 2 * core, (o + 2) % 4
    planes = [(a + 2) % 4, 3 - a, a + 1 - 2 * (a % 2), a]
    peers = [(planes[k // 4], (o + k % 4) % 4) for k in range(16) if k != 12]

    def remote(src, dst, send, recv, dest):
        return pltpu.make_async_remote_copy(src_ref=src, dst_ref=dst, send_sem=send, recv_sem=recv,
                                            device_id={'aux': dest[0], 'orb': dest[1]}, device_id_type=MESH)

    def b_copy(g):
        rows = pl.ds(g * 4, 4)
        return pltpu.make_async_copy(b_hbm.at[rows], bb.at[rows], b_sem.at[g])

    m_copy = pltpu.make_async_copy(m_hbm, mown, m_sem)
    m_copy.start()
    for g in range(AHEAD):
        b_copy(g).start()

    barrier = pltpu.get_barrier_semaphore()
    for dest in peers:
        pl.semaphore_signal(barrier, inc=1, device_id={'aux': dest[0], 'orb': dest[1]}, device_id_type=MESH)

    m_copy.wait()
    m0, m1, m2 = split3(mown[...])
    pad = jnp.zeros((32, 896), BF16)
    mall[pl.ds(a, 1), 0:224, :] = m0[None]
    mall[pl.ds(a, 1), 224:256, :] = pad[None]
    mall[4, 0:224, :] = m1
    mall[4, 224:256, :] = pad
    mall[5, 0:224, :] = m2
    mall[5, 224:256, :] = pad

    pl.semaphore_wait(barrier, 15)

    quarter = pl.ds(pl.multiple_of(o * 64, 64), 64)

    def mz_copy(plane, step):
        part = mall.at[plane, quarter, :]
        return remote(part, part, mz_send.at[plane, (step + 1) // 2], mz_recv.at[plane], (a + step, o))

    def mf_copy(plane, part_of, dest, k):
        part = mall.at[plane, pl.ds(pl.multiple_of(part_of * 64, 64), 64), :]
        return remote(part, part, mf_send.at[plane, k], mf_recv.at[plane, part_of], (a, dest))

    def relay(r, action):
        for step in (1, -1):
            plane = a - step * r

            @pl.when((plane >= 0) & (plane <= 3))
            def _():
                if action == 'send' and r > 0:
                    mz_copy(plane, step).wait_recv()
                if r < 3:
                    @pl.when((a + step >= 0) & (a + step <= 3))
                    def _():
                        cp = mz_copy(plane, step)
                        cp.start() if action == 'send' else cp.wait_send()
                if action == 'send' and r > 0:
                    mf_copy(plane, o, core_mate, 0).start()
                    mf_copy(plane, o, y_mate, 1).start()

    def pass_on(r):
        for step in (1, -1):
            plane = a - step * r

            @pl.when((plane >= 0) & (plane <= 3))
            def _():
                mf_copy(plane, y_mate, y_mate, 2).wait_recv()
                mf_copy(plane, y_mate, core_mate, 2).start()

    relay(0, 'send')

    def half_copy(ii, dest, rows):
        d = dest[0] * 4 + dest[1]
        return remote(sbuf.at[2 * d + ii, rows, :], rbuf.at[ii, me, rows, :], s_send.at[ii, d], s_recv.at[ii, me], dest)

    parts = split3(c_ref[...])
    zero = jnp.zeros((32, 320), BF16)
    for k in range(3):
        rows = [parts[k] if j <= 2 - k else zero for j in range(3)]
        c3[32 * k:32 * k + 32, :] = jnp.concatenate(rows + [zero[:, :64]], axis=1)
    own = jnp.zeros((32, 80), F32)
    for k in range(4):
        own = jnp.where(o == k, c_ref[:, 80 * k:80 * k + 80], own)
    for m in range(80):
        cb[m] = jnp.broadcast_to(own[:, m:m + 1], (32, 128))
    stage[1] = jnp.zeros((512, 128), F32)
    gam[...] = jnp.zeros((32, 256), F32)

    def group(g, carry):
        for k in range(2):
            b_copy(2 * g + k).wait()

        @pl.when(2 * g + AHEAD < 20)
        def _():
            for k in range(2):
                b_copy(2 * g + k + AHEAD).start()

        base = lax.rem(g, 2) * 8

        def rows4(k, carry):
            part0 = part1 = None
            for j in range(4):
                m = 4 * k + j
                w = jnp.concatenate(list(split3(bb[g * 8 + m])) + [jnp.zeros((64, 224), BF16)], axis=0)
                r = dot(c3[...], w)
                h = r[0:32] + r[32:64] + r[64:96]
                stage[0, pl.ds(base + m, 32, stride=16), :] = h[:, :128]
                stage[1, pl.ds(base + m, 32, stride=16), 0:96] = h[:, 128:]
                coef = cb[g * 8 + m]
                add0, add1 = h[:, :128] * coef, h[:, 128:] * coef[:, :96]
                part0 = add0 if part0 is None else part0 + add0
                part1 = add1 if part1 is None else part1 + add1
            gam[:, 0:128] += part0
            gam[:, 128:224] += part1
            return carry

        lax.fori_loop(0, 2, rows4, 0)

        @pl.when(lax.rem(g, 2) == 1)
        def _():
            rows = pl.ds(pl.multiple_of((g // 2) * 16, 16), 16)
            for t in range(2):
                sbuf[:, rows, 128 * t:128 * t + 128] = stage[t].reshape(32, 16, 128).astype(BF16)
            for dest in peers:
                half_copy(0, dest, rows).start()

        @pl.when(g == 3)
        def _():
            relay(1, 'send')

        @pl.when(g == 6)
        def _():
            relay(2, 'send')
            pass_on(1)

        return carry

    lax.fori_loop(0, 10, group, 0)

    def g_copy(dest):
        return remote(gsend, grecv.at[me], g_send.at[dest[0] * 4 + dest[1]], g_recv.at[me], dest)

    g_row = jnp.sum(gam[...], axis=0, keepdims=True)
    gsend[...] = g_row
    grecv[pl.ds(me, 1)] = g_row[None]
    for dest in peers:
        g_copy(dest).start()

    full = pl.ds(0, 80)
    for dest in peers:
        half_copy(1, dest, pl.ds(0, 48)).start()
    rbuf[:, pl.ds(me, 1)] = sbuf[pl.ds(2 * me, 2)][:, None]
    relay(3, 'send')
    pass_on(2)

    def lanes_of(rows):
        return jnp.concatenate([r[:, :224] for r in rows], axis=1)

    def as_row(col):
        x = jnp.broadcast_to(col, (224, 128))
        return jnp.concatenate([jnp.transpose(x[:128])[0:1], jnp.transpose(x[96:])[0:1, 32:], jnp.zeros((1, 32), F32)],
                               axis=1)

    def times_metric(row):
        return jnp.sum(mown[...] * row, axis=1, keepdims=True)

    for s in peers:
        remote(gsend, grecv.at[s[0] * 4 + s[1]], g_send.at[0], g_recv.at[s[0] * 4 + s[1]], s).wait_recv()
    gamma = lanes_of([grecv[4 * b] + grecv[4 * b + 1] + grecv[4 * b + 2] + grecv[4 * b + 3] for b in range(4)])
    fit_row = as_row(times_metric(gamma))
    fsend[...] = fit_row
    frecv[pl.ds(a, 1)] = fit_row[None]

    def f_copy(j):
        return remote(fsend, frecv.at[a], f_send.at[j], f_recv.at[a], (planes[j], o))

    for j in range(3):
        f_copy(j).start()
    for dest in peers:
        half_copy(1, dest, pl.ds(48, 32)).start()
    pass_on(3)

    for r in range(1, 4):
        for step in (1, -1):
            plane = a - step * r

            @pl.when((plane >= 0) & (plane <= 3))
            def _():
                for part_of in (core_mate, 3 - o):
                    mf_copy(plane, part_of, part_of, 0).wait_recv()

    def t_and_k(ii):
        for s in peers:
            n = s[0] * 4 + s[1]
            remote(sbuf.at[ii], rbuf.at[ii, n], s_send.at[ii, n], s_recv.at[ii, n], s).wait_recv()
        for n0, n1 in ((0, 256), (256, 512), (512, 768), (768, 896)):
            t = dot(rbuf[ii, 0:4].reshape(320, 256), mall[0, :, n0:n1])
            for b in range(1, 4):
                t += dot(rbuf[ii, 4 * b:4 * b + 4].reshape(320, 256), mall[b, :, n0:n1])
            mine = rbuf[ii, pl.ds(a * 4, 4)].reshape(320, 256)
            t += dot(mine, mall[4, :, n0:n1]) + dot(mine, mall[5, :, n0:n1])
            for k, h in enumerate(split3(t)):
                tt[k, :, n0:n1] = h
        t0, t1, t2 = tt[0], tt[1], tt[2]
        k = dot_nt(t0, t0) + dot_nt(t1, t1) + dot_nt(t0, t1) + dot_nt(t0, t2) + dot_nt(t1, t0) + dot_nt(t2, t0)
        if ii == 0:
            ks[...] = k
        else:
            ks[...] += k

    t_and_k(0)
    for j in range(3):
        remote(fsend, frecv.at[planes[j]], f_send.at[j], f_recv.at[planes[j]], (planes[j], o)).wait_recv()
    weights = times_metric(lanes_of([frecv[b] for b in range(4)]))
    w_row = as_row(2.0 * weights)

    lane = lax.broadcasted_iota(jnp.int32, (8, 128), 1)
    w0, w1 = jnp.broadcast_to(w_row[:, :128], (8, 128)), jnp.broadcast_to(w_row[:, 128:224], (8, 96))

    def coul(k, carry):
        rows = pl.ds(pl.multiple_of(k * 8, 8), 8)
        acc = jnp.zeros((8, 128), F32)
        for m in range(80):
            y = bb[m, rows, 0:128] * w0
            z = bb[m, rows, 128:224] * w1
            col = jnp.sum(y, axis=1, keepdims=True) + jnp.sum(z, axis=1, keepdims=True)
            acc = jnp.where(lane == m, col, acc)
        jacc[rows, :] = acc[:, :80]
        return carry

    lax.fori_loop(0, 40, coul, 0)
    jt = jnp.transpose(jacc[...])

    t_and_k(1)

    def packed(x):
        tail = jnp.concatenate([x[56:, :48], jnp.concatenate([x[56:, 48:], jnp.zeros((24, 16), F32)], axis=1),
                                jnp.zeros((8, 48), F32)], axis=0)
        return jnp.concatenate([x[:56], tail], axis=1)

    for c in range(4):
        for k in range(4):
            gs[k % 2, k // 2, c] = packed(jnp.where(o == k, jt[:, 80 * c:80 * c + 80], 0.0)
                                          - ks[80 * k:80 * k + 80, 80 * c:80 * c + 80])
    pair = remote(gs.at[1 - core], gp, p_sems.at[0], p_sems.at[1], (a, core_mate))
    pair.start()
    pair.wait()
    gf[...] = gs[core] + gp[...]

    def r_copy(k):
        plane, y = planes[k // 2], (row_y + k % 2) % 2
        return remote(gf.at[y, plane], gr.at[a, row_y], r_send.at[k], r_recv.at[a, row_y], (plane, 2 * y + core))

    r_order = (0, 1, 2, 3, 4, 5, 7)
    for k in r_order:
        r_copy(k).start()
    total = gf[row_y, a]
    for k in r_order:
        plane, y = planes[k // 2], (row_y + k % 2) % 2
        remote(gf.at[y, plane], gr.at[plane, y], r_send.at[k], r_recv.at[plane, y], (plane, 2 * y + core)).wait_recv()
        total = total + gr[plane, y]
    out_ref[0] = jnp.concatenate([total[:, :80], jnp.concatenate([total[0:24, 80:128], total[24:48, 80:112]], axis=1)], axis=0)


    for dest in peers:
        half_copy(0, dest, full).wait_send()
        half_copy(1, dest, full).wait_send()
        g_copy(dest).wait_send()
    for k in r_order:
        r_copy(k).wait_send()
    for r in range(3):
        relay(r, 'drain')
    for j in range(3):
        f_copy(j).wait_send()
        for k in range(3):
            mf_copy(planes[j], o, o, k).wait_send()


def solution(mesh):
    def local_fock(ints_blk, metric_blk, orbitals):
        dma = pltpu.SemaphoreType.DMA
        return pl.pallas_call(
            kernel,
            name='fock',
            out_shape=jax.ShapeDtypeStruct((1, 80, 80), F32),
            in_specs=[pl.BlockSpec(memory_space=pl.ANY), pl.BlockSpec(memory_space=pl.ANY),
                      pl.BlockSpec(memory_space=pltpu.VMEM)],
            out_specs=pl.BlockSpec(memory_space=pltpu.VMEM),
            scratch_shapes=[
                pltpu.VMEM((80, 320, 224), F32),
                pltpu.VMEM((2, 512, 128), F32),
                pltpu.VMEM((32, 80, 256), BF16),
                pltpu.VMEM((2, 16, 80, 256), BF16),
                pltpu.VMEM((6, 256, 896), BF16),
                pltpu.VMEM((224, 896), F32),
                pltpu.VMEM((80, 32, 128), F32),
                pltpu.VMEM((96, 1024), BF16),
                pltpu.VMEM((3, 320, 896), BF16),
                pltpu.VMEM((320, 320), F32),
                pltpu.VMEM((320, 80), F32),
                pltpu.VMEM((32, 256), F32),
                pltpu.VMEM((1, 256), F32),
                pltpu.VMEM((16, 1, 256), F32),
                pltpu.VMEM((1, 256), F32),
                pltpu.VMEM((4, 1, 256), F32),
                pltpu.VMEM((2, 2, 4, 56, 128), F32),
                pltpu.VMEM((2, 4, 56, 128), F32),
                pltpu.VMEM((2, 4, 56, 128), F32),
                pltpu.VMEM((4, 2, 56, 128), F32),
                dma((20,)), dma(()),
                dma((2, 16)), dma((2, 16)),
                dma((4, 2)), dma((4,)),
                dma((4, 3)), dma((4, 4)),
                dma((16,)), dma((16,)),
                dma((3,)), dma((4,)),
                dma((2,)), dma((8,)), dma((4, 2)),
            ],
            compiler_params=pltpu.CompilerParams(collective_id=0, has_side_effects=True, vmem_limit_bytes=67043328),
        )(jnp.transpose(ints_blk, (1, 2, 0)), metric_blk, jnp.transpose(orbitals[0]))

    return jax.shard_map(local_fock, mesh=mesh, in_specs=(P(('sys', 'aux'), 'orb', None), P(('sys', 'aux'), None), P('sys', None, None)), out_specs=P('sys', 'orb', 'aux'), check_vma=False)
```

time: 85.5 us -> 67.5 us (0.79); the launches traced: 84.1 us -> 67.2 us
  Pallas kernels: 82.7 us -> 65.8 us
    pallas_call x1, Pallas kernels: 82.7 us -> 65.8 us  [local_fock(): pl.pallas_call(kernel, name='fock', out_shape=jax.ShapeDtypeStruct((1, 80...]
where the time goes in v4:
time: 67.5 us; the launch traced here: 67.2 us
  Pallas kernels  65.8 us (97%)
  local copies, waits for them, and re-layouts  1.4 us (2%)
    pallas_call x1, Pallas kernels, local_fock(): pl.pallas_call(kernel, name='fock', out_shape=jax.ShapeDtypeStruct((1, 80...  65.8 us
    unnamed x1, local copies, waits for them, and re-layouts  1.4 us

profile of v4, /device:TPU:0, one launch (start us, length us, event | category | flops | bytes accessed | tf_op | source)
XLA Modules:
  0.0 67.2 jit_solution(11852937627203153361)
XLA Ops:
  0.0 65.8 %fock.1 = f32[1,80,80]{2,1,0:T(8,128)} custom-call(f32[80,320,224]{2,1,0:T(8,128)} %bitcast.4, f32[224,896]{1,0:T(8,128)} %m_hbm.1, f32[32,320]{1,0:T(8,128)} %bitcast.5), custom_call_target="tpu_custom_call" | custom-call | tf_op jit(solution)/shard_map/fock/pallas_call | solution.py:319
  65.8 1.4 %copy.5 = f32[1,80,80]{2,1,0:T(8,128)} copy(f32[1,80,80]{2,1,0:T(8,128)} %fock.1) | data formatting | bytes 51200

commit v5 on v4

--- a/solution.py
+++ b/solution.py
@@ -10,7 +10,7 @@
 F32, BF16 = jnp.float32, jnp.bfloat16
 MESH = pl.DeviceIdType.MESH
 NT = (((1,), (1,)), ((), ()))
-AHEAD = 4
+AHEAD = 8
 
 
 def split3(x):
@@ -29,7 +29,7 @@
     return lax.dot_general(a, b, NT, preferred_element_type=F32)
 
 
-def kernel(b_hbm, m_hbm, c_ref, out_ref, bb, stage, sbuf, rbuf, mall, mown, cb, c3, tt, ks, jacc, gam, gsend, grecv,
+def kernel(b_hbm, m_hbm, c_ref, out_ref, bb, stage, sbuf, rbuf, mall, mown, cb, c3, tt, ks, kx, jacc, gam, gsend, grecv,
            fsend, frecv, gs, gp, gf, gr, b_sem, m_sem, s_send, s_recv, mz_send, mz_recv, mf_send, mf_recv, g_send, g_recv,
            f_send, f_recv, p_sems, r_send, r_recv):
     a, o = lax.axis_index('aux'), lax.axis_index('orb')
@@ -161,11 +161,11 @@
             for dest in peers:
                 half_copy(0, dest, rows).start()
 
-        @pl.when(g == 3)
+        @pl.when(g == 1)
         def _():
             relay(1, 'send')
 
-        @pl.when(g == 6)
+        @pl.when(g == 4)
         def _():
             relay(2, 'send')
             pass_on(1)
@@ -239,11 +239,14 @@
             for k, h in enumerate(split3(t)):
                 tt[k, :, n0:n1] = h
         t0, t1, t2 = tt[0], tt[1], tt[2]
-        k = dot_nt(t0, t0) + dot_nt(t1, t1) + dot_nt(t0, t1) + dot_nt(t0, t2) + dot_nt(t1, t0) + dot_nt(t2, t0)
+        same = dot_nt(t0, t0) + dot_nt(t1, t1)
+        cross = dot_nt(t0, t1) + dot_nt(t0, t2)
         if ii == 0:
-            ks[...] = k
+            ks[...] = same
+            kx[...] = cross
         else:
-            ks[...] += k
+            cross = kx[...] + cross
+            ks[...] += same + cross + jnp.transpose(cross)
 
     t_and_k(0)
     for j in range(3):
@@ -254,13 +257,14 @@
     lane = lax.broadcasted_iota(jnp.int32, (8, 128), 1)
     w0, w1 = jnp.broadcast_to(w_row[:, :128], (8, 128)), jnp.broadcast_to(w_row[:, 128:224], (8, 96))
 
+    zero32 = jnp.zeros((8, 32), F32)
+
     def coul(k, carry):
         rows = pl.ds(pl.multiple_of(k * 8, 8), 8)
         acc = jnp.zeros((8, 128), F32)
         for m in range(80):
-            y = bb[m, rows, 0:128] * w0
-            z = bb[m, rows, 128:224] * w1
-            col = jnp.sum(y, axis=1, keepdims=True) + jnp.sum(z, axis=1, keepdims=True)
+            z = jnp.concatenate([bb[m, rows, 128:224] * w1, zero32], axis=1)
+            col = jnp.sum(bb[m, rows, 0:128] * w0 + z, axis=1, keepdims=True)
             acc = jnp.where(lane == m, col, acc)
         jacc[rows, :] = acc[:, :80]
         return carry
@@ -334,6 +338,7 @@
                 pltpu.VMEM((96, 1024), BF16),
                 pltpu.VMEM((3, 320, 896), BF16),
                 pltpu.VMEM((320, 320), F32),
+                pltpu.VMEM((320, 320), F32),
                 pltpu.VMEM((320, 80), F32),
                 pltpu.VMEM((32, 256), F32),
                 pltpu.VMEM((1, 256), F32),

time: 67.5 us -> 64 us (0.948)
  Pallas kernels: 65.8 us -> 62.4 us
    pallas_call x1, Pallas kernels: 65.8 us -> 62.4 us  [local_fock(): pl.pallas_call(kernel, name='fock', out_shape=jax.ShapeDtypeStruct((1, 80...]
where the time goes in v5:
time: 64 us; the launch traced here: 63.8 us
  Pallas kernels  62.4 us (98%)
  local copies, waits for them, and re-layouts  1.4 us (2%)
    pallas_call x1, Pallas kernels, local_fock(): pl.pallas_call(kernel, name='fock', out_shape=jax.ShapeDtypeStruct((1, 80...  62.4 us
    unnamed x1, local copies, waits for them, and re-layouts  1.4 us

profile of v5, /device:TPU:0, one launch (start us, length us, event | category | flops | bytes accessed | tf_op | source)
XLA Modules:
  0.0 63.8 jit_solution(5430498318923284669)
XLA Ops:
  0.0 62.4 %fock.1 = f32[1,80,80]{2,1,0:T(8,128)} custom-call(f32[80,320,224]{2,1,0:T(8,128)} %bitcast.4, f32[224,896]{1,0:T(8,128)} %m_hbm.1, f32[32,320]{1,0:T(8,128)} %bitcast.5), custom_call_target="tpu_custom_call" | custom-call | tf_op jit(solution)/shard_map/fock/pallas_call | solution.py:323
  62.4 1.4 %copy.5 = f32[1,80,80]{2,1,0:T(8,128)} copy(f32[1,80,80]{2,1,0:T(8,128)} %fock.1) | data formatting | bytes 51200

commit v6 on v5

--- a/solution.py
+++ b/solution.py
@@ -49,7 +49,7 @@
 
     m_copy = pltpu.make_async_copy(m_hbm, mown, m_sem)
     m_copy.start()
-    for g in range(AHEAD):
+    for g in range(2):
         b_copy(g).start()
 
     barrier = pltpu.get_barrier_semaphore()
@@ -57,6 +57,8 @@
         pl.semaphore_signal(barrier, inc=1, device_id={'aux': dest[0], 'orb': dest[1]}, device_id_type=MESH)
 
     m_copy.wait()
+    for g in range(2, AHEAD):
+        b_copy(g).start()
     m0, m1, m2 = split3(mown[...])
     pad = jnp.zeros((32, 896), BF16)
     mall[pl.ds(a, 1), 0:224, :] = m0[None]
@@ -161,18 +163,15 @@
             for dest in peers:
                 half_copy(0, dest, rows).start()
 
-        @pl.when(g == 1)
+        @pl.when(g == 5)
         def _():
             relay(1, 'send')
 
-        @pl.when(g == 4)
-        def _():
-            relay(2, 'send')
-            pass_on(1)
-
         return carry
 
     lax.fori_loop(0, 10, group, 0)
+    relay(2, 'send')
+    pass_on(1)
 
     def g_copy(dest):
         return remote(gsend, grecv.at[me], g_send.at[dest[0] * 4 + dest[1]], g_recv.at[me], dest)
@@ -185,7 +184,7 @@
 
     full = pl.ds(0, 80)
     for dest in peers:
-        half_copy(1, dest, pl.ds(0, 48)).start()
+        half_copy(1, dest, pl.ds(0, 16)).start()
     rbuf[:, pl.ds(me, 1)] = sbuf[pl.ds(2 * me, 2)][:, None]
     relay(3, 'send')
     pass_on(2)
@@ -214,7 +213,7 @@
     for j in range(3):
         f_copy(j).start()
     for dest in peers:
-        half_copy(1, dest, pl.ds(48, 32)).start()
+        half_copy(1, dest, pl.ds(16, 64)).start()
     pass_on(3)
 
     for r in range(1, 4):
@@ -260,16 +259,17 @@
     zero32 = jnp.zeros((8, 32), F32)
 
     def coul(k, carry):
-        rows = pl.ds(pl.multiple_of(k * 8, 8), 8)
-        acc = jnp.zeros((8, 128), F32)
-        for m in range(80):
-            z = jnp.concatenate([bb[m, rows, 128:224] * w1, zero32], axis=1)
-            col = jnp.sum(bb[m, rows, 0:128] * w0 + z, axis=1, keepdims=True)
-            acc = jnp.where(lane == m, col, acc)
-        jacc[rows, :] = acc[:, :80]
+        for j in range(4):
+            rows = pl.ds(pl.multiple_of(k * 32 + 8 * j, 8), 8)
+            acc = jnp.zeros((8, 128), F32)
+            for m in range(80):
+                z = jnp.concatenate([bb[m, rows, 128:224] * w1, zero32], axis=1)
+                col = jnp.sum(bb[m, rows, 0:128] * w0 + z, axis=1, keepdims=True)
+                acc = jnp.where(lane == m, col, acc)
+            jacc[rows, :] = acc[:, :80]
         return carry
 
-    lax.fori_loop(0, 40, coul, 0)
+    lax.fori_loop(0, 10, coul, 0)
     jt = jnp.transpose(jacc[...])
 
     t_and_k(1)

time: 64 us -> 61.4 us (0.959)
  Pallas kernels: 62.4 us -> 59.8 us
    pallas_call x1, Pallas kernels: 62.4 us -> 59.8 us  [local_fock(): pl.pallas_call(kernel, name='fock', out_shape=jax.ShapeDtypeStruct((1, 80...]
where the time goes in v6:
time: 61.4 us; the launch traced here: 61.2 us
  Pallas kernels  59.8 us (97%)
  local copies, waits for them, and re-layouts  1.4 us (2%)
    pallas_call x1, Pallas kernels, local_fock(): pl.pallas_call(kernel, name='fock', out_shape=jax.ShapeDtypeStruct((1, 80...  59.8 us
    unnamed x1, local copies, waits for them, and re-layouts  1.4 us

profile of v6, /device:TPU:0, one launch (start us, length us, event | category | flops | bytes accessed | tf_op | source)
XLA Modules:
  0.0 61.2 jit_solution(3920331493981389186)
XLA Ops:
  0.0 59.8 %fock.1 = f32[1,80,80]{2,1,0:T(8,128)} custom-call(f32[80,320,224]{2,1,0:T(8,128)} %bitcast.4, f32[224,896]{1,0:T(8,128)} %m_hbm.1, f32[32,320]{1,0:T(8,128)} %bitcast.5), custom_call_target="tpu_custom_call" | custom-call | tf_op jit(solution)/shard_map/fock/pallas_call | solution.py:323
  59.8 1.4 %copy.5 = f32[1,80,80]{2,1,0:T(8,128)} copy(f32[1,80,80]{2,1,0:T(8,128)} %fock.1) | data formatting | bytes 51200

commit v7 on v6

--- a/solution.py
+++ b/solution.py
@@ -29,7 +29,7 @@
     return lax.dot_general(a, b, NT, preferred_element_type=F32)
 
 
-def kernel(b_hbm, m_hbm, c_ref, out_ref, bb, stage, sbuf, rbuf, mall, mown, cb, c3, tt, ks, kx, jacc, gam, gsend, grecv,
+def kernel(b_hbm, m_hbm, c_ref, out_ref, bb, stage, smain, srest, rmain, rrest, rest, mall, mown, cb, c3, tt, ks, kx, jacc, gam, gsend, grecv,
            fsend, frecv, gs, gp, gf, gr, b_sem, m_sem, s_send, s_recv, mz_send, mz_recv, mf_send, mf_recv, g_send, g_recv,
            f_send, f_recv, p_sems, r_send, r_recv):
     a, o = lax.axis_index('aux'), lax.axis_index('orb')
@@ -108,9 +108,13 @@
 
     relay(0, 'send')
 
-    def half_copy(ii, dest, rows):
+    def main_copy(dest, rows):
         d = dest[0] * 4 + dest[1]
-        return remote(sbuf.at[2 * d + ii, rows, :], rbuf.at[ii, me, rows, :], s_send.at[ii, d], s_recv.at[ii, me], dest)
+        return remote(smain.at[pl.ds(2 * d, 2), rows, :], rmain.at[:, me, rows, :], s_send.at[2, d], s_recv.at[2, me], dest)
+
+    def rest_copy(ii, dest):
+        d = dest[0] * 4 + dest[1]
+        return remote(srest.at[2 * d + ii], rrest.at[ii, me], s_send.at[ii, d], s_recv.at[ii, me], dest)
 
     parts = split3(c_ref[...])
     zero = jnp.zeros((32, 320), BF16)
@@ -122,7 +126,8 @@
         own = jnp.where(o == k, c_ref[:, 80 * k:80 * k + 80], own)
     for m in range(80):
         cb[m] = jnp.broadcast_to(own[:, m:m + 1], (32, 128))
-    stage[1] = jnp.zeros((512, 128), F32)
+    rest[...] = jnp.zeros((16, 80, 128), BF16)
+    srest[:, :, 384:512] = jnp.zeros((32, 16, 128), BF16)
     gam[...] = jnp.zeros((32, 256), F32)
 
     def group(g, carry):
@@ -158,10 +163,15 @@
         @pl.when(lax.rem(g, 2) == 1)
         def _():
             rows = pl.ds(pl.multiple_of((g // 2) * 16, 16), 16)
-            for t in range(2):
-                sbuf[:, rows, 128 * t:128 * t + 128] = stage[t].reshape(32, 16, 128).astype(BF16)
+            smain[:, rows, :] = stage[0].reshape(32, 16, 128).astype(BF16)
             for dest in peers:
-                half_copy(0, dest, rows).start()
+                main_copy(dest, rows).start()
+
+        for c in range(5):
+            @pl.when(g == 2 * c + 1)
+            def _():
+                at = 96 * c if c < 4 else 384
+                srest[:, :, at:at + 96] = stage[1].reshape(32, 16, 128)[:, :, :96].astype(BF16)
 
         @pl.when(g == 5)
         def _():
@@ -182,10 +192,10 @@
     for dest in peers:
         g_copy(dest).start()
 
-    full = pl.ds(0, 80)
-    for dest in peers:
-        half_copy(1, dest, pl.ds(0, 16)).start()
-    rbuf[:, pl.ds(me, 1)] = sbuf[pl.ds(2 * me, 2)][:, None]
+    for dest in peers:
+        rest_copy(0, dest).start()
+    rmain[:, pl.ds(me, 1)] = smain[pl.ds(2 * me, 2)][:, None]
+    rrest[:, pl.ds(me, 1)] = srest[pl.ds(2 * me, 2)][:, None]
     relay(3, 'send')
     pass_on(2)
 
@@ -213,7 +223,7 @@
     for j in range(3):
         f_copy(j).start()
     for dest in peers:
-        half_copy(1, dest, pl.ds(16, 64)).start()
+        rest_copy(1, dest).start()
     pass_on(3)
 
     for r in range(1, 4):
@@ -228,12 +238,23 @@
     def t_and_k(ii):
         for s in peers:
             n = s[0] * 4 + s[1]
-            remote(sbuf.at[ii], rbuf.at[ii, n], s_send.at[ii, n], s_recv.at[ii, n], s).wait_recv()
+            if ii == 0:
+                remote(smain.at[pl.ds(0, 2)], rmain.at[:, n], s_send.at[2, n], s_recv.at[2, n], s).wait_recv()
+            remote(srest.at[ii], rrest.at[ii, n], s_send.at[ii, n], s_recv.at[ii, n], s).wait_recv()
+        for n in range(16):
+            for c in range(5):
+                at = 96 * c if c < 4 else 384
+                rest[n, 16 * c:16 * c + 16, 0:96] = rrest[ii, n, :, at:at + 96]
+
+        def rows_of(plane):
+            four = pl.ds(4 * plane, 4)
+            return jnp.concatenate([rmain[ii, four].reshape(320, 128), rest[four].reshape(320, 128)], axis=1)
+
         for n0, n1 in ((0, 256), (256, 512), (512, 768), (768, 896)):
-            t = dot(rbuf[ii, 0:4].reshape(320, 256), mall[0, :, n0:n1])
+            t = dot(rows_of(0), mall[0, :, n0:n1])
             for b in range(1, 4):
-                t += dot(rbuf[ii, 4 * b:4 * b + 4].reshape(320, 256), mall[b, :, n0:n1])
-            mine = rbuf[ii, pl.ds(a * 4, 4)].reshape(320, 256)
+                t += dot(rows_of(b), mall[b, :, n0:n1])
+            mine = rows_of(a)
             t += dot(mine, mall[4, :, n0:n1]) + dot(mine, mall[5, :, n0:n1])
             for k, h in enumerate(split3(t)):
                 tt[k, :, n0:n1] = h
@@ -304,8 +325,9 @@
 
 
     for dest in peers:
-        half_copy(0, dest, full).wait_send()
-        half_copy(1, dest, full).wait_send()
+        main_copy(dest, pl.ds(0, 80)).wait_send()
+        rest_copy(0, dest).wait_send()
+        rest_copy(1, dest).wait_send()
         g_copy(dest).wait_send()
     for k in r_order:
         r_copy(k).wait_send()
@@ -330,8 +352,11 @@
             scratch_shapes=[
                 pltpu.VMEM((80, 320, 224), F32),
                 pltpu.VMEM((2, 512, 128), F32),
-                pltpu.VMEM((32, 80, 256), BF16),
-                pltpu.VMEM((2, 16, 80, 256), BF16),
+                pltpu.VMEM((32, 80, 128), BF16),
+                pltpu.VMEM((32, 16, 512), BF16),
+                pltpu.VMEM((2, 16, 80, 128), BF16),
+                pltpu.VMEM((2, 16, 16, 512), BF16),
+                pltpu.VMEM((16, 80, 128), BF16),
                 pltpu.VMEM((6, 256, 896), BF16),
                 pltpu.VMEM((224, 896), F32),
                 pltpu.VMEM((80, 32, 128), F32),
@@ -350,7 +375,7 @@
                 pltpu.VMEM((2, 4, 56, 128), F32),
                 pltpu.VMEM((4, 2, 56, 128), F32),
                 dma((20,)), dma(()),
-                dma((2, 16)), dma((2, 16)),
+                dma((3, 16)), dma((3, 16)),
                 dma((4, 2)), dma((4,)),
                 dma((4, 3)), dma((4, 4)),
                 dma((16,)), dma((16,)),

time: 61.4 us -> 63.9 us (1.041); the launches traced: 61.2 us -> 62.9 us
  Pallas kernels: 59.8 us -> 61.5 us
    pallas_call x1, Pallas kernels: 59.8 us -> 61.5 us  [local_fock(): pl.pallas_call(kernel, name='fock', out_shape=jax.ShapeDtypeStruct((1, 80...]
where the time goes in v7:
time: 63.9 us; the launch traced here: 62.9 us
  Pallas kernels  61.5 us (96%)
  local copies, waits for them, and re-layouts  1.4 us (2%)
    pallas_call x1, Pallas kernels, local_fock(): pl.pallas_call(kernel, name='fock', out_shape=jax.ShapeDtypeStruct((1, 80...  61.5 us
    unnamed x1, local copies, waits for them, and re-layouts  1.4 us

profile of v7, /device:TPU:0, one launch (start us, length us, event | category | flops | bytes accessed | tf_op | source)
XLA Modules:
  0.0 62.9 jit_solution(7046710966767919366)
XLA Ops:
  0.0 61.5 %fock.1 = f32[1,80,80]{2,1,0:T(8,128)} custom-call(f32[80,320,224]{2,1,0:T(8,128)} %bitcast.4, f32[224,896]{1,0:T(8,128)} %m_hbm.1, f32[32,320]{1,0:T(8,128)} %bitcast.5), custom_call_target="tpu_custom_call" | custom-call | tf_op jit(solution)/shard_map/fock/pallas_call | solution.py:345
  61.5 1.4 %copy.5 = f32[1,80,80]{2,1,0:T(8,128)} copy(f32[1,80,80]{2,1,0:T(8,128)} %fock.1) | data formatting | bytes 51200

commit v8 on v7

--- a/solution.py
+++ b/solution.py
@@ -108,9 +108,10 @@
 
     relay(0, 'send')
 
-    def main_copy(dest, rows):
+    def main_copy(ii, dest, rows):
         d = dest[0] * 4 + dest[1]
-        return remote(smain.at[pl.ds(2 * d, 2), rows, :], rmain.at[:, me, rows, :], s_send.at[2, d], s_recv.at[2, me], dest)
+        return remote(smain.at[2 * d + ii, rows, :], rmain.at[ii, me, rows, :], s_send.at[2 + ii, d], s_recv.at[2 + ii, me],
+                      dest)
 
     def rest_copy(ii, dest):
         d = dest[0] * 4 + dest[1]
@@ -165,7 +166,7 @@
             rows = pl.ds(pl.multiple_of((g // 2) * 16, 16), 16)
             smain[:, rows, :] = stage[0].reshape(32, 16, 128).astype(BF16)
             for dest in peers:
-                main_copy(dest, rows).start()
+                main_copy(0, dest, rows).start()
 
         for c in range(5):
             @pl.when(g == 2 * c + 1)
@@ -173,15 +174,13 @@
                 at = 96 * c if c < 4 else 384
                 srest[:, :, at:at + 96] = stage[1].reshape(32, 16, 128)[:, :, :96].astype(BF16)
 
-        @pl.when(g == 5)
+        @pl.when(g == 4)
         def _():
             relay(1, 'send')
 
         return carry
 
     lax.fori_loop(0, 10, group, 0)
-    relay(2, 'send')
-    pass_on(1)
 
     def g_copy(dest):
         return remote(gsend, grecv.at[me], g_send.at[dest[0] * 4 + dest[1]], g_recv.at[me], dest)
@@ -194,10 +193,12 @@
 
     for dest in peers:
         rest_copy(0, dest).start()
+    relay(2, 'send')
+    pass_on(1)
+    for dest in peers:
+        main_copy(1, dest, pl.ds(0, 32)).start()
     rmain[:, pl.ds(me, 1)] = smain[pl.ds(2 * me, 2)][:, None]
     rrest[:, pl.ds(me, 1)] = srest[pl.ds(2 * me, 2)][:, None]
-    relay(3, 'send')
-    pass_on(2)
 
     def lanes_of(rows):
         return jnp.concatenate([r[:, :224] for r in rows], axis=1)
@@ -223,7 +224,10 @@
     for j in range(3):
         f_copy(j).start()
     for dest in peers:
+        main_copy(1, dest, pl.ds(32, 48)).start()
         rest_copy(1, dest).start()
+    relay(3, 'send')
+    pass_on(2)
     pass_on(3)
 
     for r in range(1, 4):
@@ -238,8 +242,7 @@
     def t_and_k(ii):
         for s in peers:
             n = s[0] * 4 + s[1]
-            if ii == 0:
-                remote(smain.at[pl.ds(0, 2)], rmain.at[:, n], s_send.at[2, n], s_recv.at[2, n], s).wait_recv()
+            remote(smain.at[ii], rmain.at[ii, n], s_send.at[2 + ii, n], s_recv.at[2 + ii, n], s).wait_recv()
             remote(srest.at[ii], rrest.at[ii, n], s_send.at[ii, n], s_recv.at[ii, n], s).wait_recv()
         for n in range(16):
             for c in range(5):
@@ -325,7 +328,8 @@
 
 
     for dest in peers:
-        main_copy(dest, pl.ds(0, 80)).wait_send()
+        main_copy(0, dest, pl.ds(0, 80)).wait_send()
+        main_copy(1, dest, pl.ds(0, 80)).wait_send()
         rest_copy(0, dest).wait_send()
         rest_copy(1, dest).wait_send()
         g_copy(dest).wait_send()
@@ -375,7 +379,7 @@
                 pltpu.VMEM((2, 4, 56, 128), F32),
                 pltpu.VMEM((4, 2, 56, 128), F32),
                 dma((20,)), dma(()),
-                dma((3, 16)), dma((3, 16)),
+                dma((4, 16)), dma((4, 16)),
                 dma((4, 2)), dma((4,)),
                 dma((4, 3)), dma((4, 4)),
                 dma((16,)), dma((16,)),

time: 63.9 us -> 59.1 us (0.925); the launches traced: 62.9 us -> 58.9 us
  Pallas kernels: 61.5 us -> 57.5 us
    pallas_call x1, Pallas kernels: 61.5 us -> 57.5 us  [local_fock(): pl.pallas_call(kernel, name='fock', out_shape=jax.ShapeDtypeStruct((1, 80...]
where the time goes in v8:
time: 59.1 us; the launch traced here: 58.9 us
  Pallas kernels  57.5 us (97%)
  local copies, waits for them, and re-layouts  1.4 us (2%)
    pallas_call x1, Pallas kernels, local_fock(): pl.pallas_call(kernel, name='fock', out_shape=jax.ShapeDtypeStruct((1, 80...  57.5 us
    unnamed x1, local copies, waits for them, and re-layouts  1.4 us

profile of v8, /device:TPU:0, one launch (start us, length us, event | category | flops | bytes accessed | tf_op | source)
XLA Modules:
  0.0 58.9 jit_solution(2289475558488921617)
XLA Ops:
  0.0 57.5 %fock.1 = f32[1,80,80]{2,1,0:T(8,128)} custom-call(f32[80,320,224]{2,1,0:T(8,128)} %bitcast.4, f32[224,896]{1,0:T(8,128)} %m_hbm.1, f32[32,320]{1,0:T(8,128)} %bitcast.5), custom_call_target="tpu_custom_call" | custom-call | tf_op jit(solution)/shard_map/fock/pallas_call | solution.py:349
  57.5 1.4 %copy.5 = f32[1,80,80]{2,1,0:T(8,128)} copy(f32[1,80,80]{2,1,0:T(8,128)} %fock.1) | data formatting | bytes 51200

commit v9 on v8

--- a/solution.py
+++ b/solution.py
@@ -307,18 +307,23 @@
         for k in range(4):
             gs[k % 2, k // 2, c] = packed(jnp.where(o == k, jt[:, 80 * c:80 * c + 80], 0.0)
                                           - ks[80 * k:80 * k + 80, 80 * c:80 * c + 80])
-    pair = remote(gs.at[1 - core], gp, p_sems.at[0], p_sems.at[1], (a, core_mate))
-    pair.start()
-    pair.wait()
-    gf[...] = gs[core] + gp[...]
+    far = 2 * (1 - a // 2)
+    halves = [pl.ds(far, 2), pl.ds(2 - far, 2)]
+    pairs = [remote(gs.at[1 - core, :, half], gp.at[:, half], p_sems.at[0, k], p_sems.at[1, k], (a, core_mate))
+             for k, half in enumerate(halves)]
+    for cp in pairs:
+        cp.start()
 
     def r_copy(k):
         plane, y = planes[k // 2], (row_y + k % 2) % 2
         return remote(gf.at[y, plane], gr.at[a, row_y], r_send.at[k], r_recv.at[a, row_y], (plane, 2 * y + core))
 
     r_order = (0, 1, 2, 3, 4, 5, 7)
-    for k in r_order:
-        r_copy(k).start()
+    for j, half in enumerate(halves):
+        pairs[j].wait()
+        gf[:, half] = gs[core, :, half] + gp[:, half]
+        for k in r_order[4 * j:4 * j + 4]:
+            r_copy(k).start()
     total = gf[row_y, a]
     for k in r_order:
         plane, y = planes[k // 2], (row_y + k % 2) % 2
@@ -384,7 +389,7 @@
                 dma((4, 3)), dma((4, 4)),
                 dma((16,)), dma((16,)),
                 dma((3,)), dma((4,)),
-                dma((2,)), dma((8,)), dma((4, 2)),
+                dma((2, 2)), dma((8,)), dma((4, 2)),
             ],
             compiler_params=pltpu.CompilerParams(collective_id=0, has_side_effects=True, vmem_limit_bytes=67043328),
         )(jnp.transpose(ints_blk, (1, 2, 0)), metric_blk, jnp.transpose(orbitals[0]))

time: 59.1 us -> 58.9 us (level)
  no operation moved by 1% of the time
where the time goes in v9:
time: 58.9 us; the launch traced here: 58.7 us
  Pallas kernels  57.3 us (97%)
  local copies, waits for them, and re-layouts  1.4 us (2%)
    pallas_call x1, Pallas kernels, local_fock(): pl.pallas_call(kernel, name='fock', out_shape=jax.ShapeDtypeStruct((1, 80...  57.3 us
    unnamed x1, local copies, waits for them, and re-layouts  1.4 us

profile of v9, /device:TPU:0, one launch (start us, length us, event | category | flops | bytes accessed | tf_op | source)
XLA Modules:
  0.0 58.7 jit_solution(734375423528196526)
XLA Ops:
  0.0 57.3 %fock.1 = f32[1,80,80]{2,1,0:T(8,128)} custom-call(f32[80,320,224]{2,1,0:T(8,128)} %bitcast.4, f32[224,896]{1,0:T(8,128)} %m_hbm.1, f32[32,320]{1,0:T(8,128)} %bitcast.5), custom_call_target="tpu_custom_call" | custom-call | tf_op jit(solution)/shard_map/fock/pallas_call | solution.py:354
  57.3 1.4 %copy.5 = f32[1,80,80]{2,1,0:T(8,128)} copy(f32[1,80,80]{2,1,0:T(8,128)} %fock.1) | data formatting | bytes 51200

commit v10 on v9

--- a/solution.py
+++ b/solution.py
@@ -195,8 +195,6 @@
         rest_copy(0, dest).start()
     relay(2, 'send')
     pass_on(1)
-    for dest in peers:
-        main_copy(1, dest, pl.ds(0, 32)).start()
     rmain[:, pl.ds(me, 1)] = smain[pl.ds(2 * me, 2)][:, None]
     rrest[:, pl.ds(me, 1)] = srest[pl.ds(2 * me, 2)][:, None]
 
@@ -224,7 +222,7 @@
     for j in range(3):
         f_copy(j).start()
     for dest in peers:
-        main_copy(1, dest, pl.ds(32, 48)).start()
+        main_copy(1, dest, pl.ds(0, 80)).start()
         rest_copy(1, dest).start()
     relay(3, 'send')
     pass_on(2)

time: 58.9 us -> 58.9 us (level)
  no operation moved by 1% of the time
where the time goes in v10:
time: 58.9 us; the launch traced here: 58.7 us
  Pallas kernels  57.2 us (97%)
  local copies, waits for them, and re-layouts  1.4 us (2%)
    pallas_call x1, Pallas kernels, local_fock(): pl.pallas_call(kernel, name='fock', out_shape=jax.ShapeDtypeStruct((1, 80...  57.2 us
    unnamed x1, local copies, waits for them, and re-layouts  1.4 us

profile of v10, /device:TPU:0, one launch (start us, length us, event | category | flops | bytes accessed | tf_op | source)
XLA Modules:
  0.0 58.7 jit_solution(2414469203486899062)
XLA Ops:
  0.0 57.2 %fock.1 = f32[1,80,80]{2,1,0:T(8,128)} custom-call(f32[80,320,224]{2,1,0:T(8,128)} %bitcast.4, f32[224,896]{1,0:T(8,128)} %m_hbm.1, f32[32,320]{1,0:T(8,128)} %bitcast.5), custom_call_target="tpu_custom_call" | custom-call | tf_op jit(solution)/shard_map/fock/pallas_call | solution.py:352
  57.3 1.4 %copy.5 = f32[1,80,80]{2,1,0:T(8,128)} copy(f32[1,80,80]{2,1,0:T(8,128)} %fock.1) | data formatting | bytes 51200
